TPU v7x, 256 devices: a whole 4x4x8 slice. The times are simulated.
256 devices in a mesh: row: 16 (over x, z_lo, core), col: 16 (over z_hi, y).
Axes of the slice: x: 4, y: 4, z: 8 (z_hi: 4, z_lo: 2; z = z_hi * 2 + z_lo), core: 2. Of those that a mesh axis runs over, the one named last changes fastest.
Arguments:
- tokens: bfloat16 [2048, 4096], P('col', 'row'), may hold values from -12 to 12
- target: bfloat16 [2048, 4096], P('col', 'row'), may hold values from -6 to 6
- gate_weight: bfloat16 [4096, 5504], P('row', 'col'), may hold values from -0.09375 to 0.09375
- up_weight: bfloat16 [4096, 5504], P('row', 'col'), may hold values from -0.09375 to 0.09375
- down_weight: bfloat16 [5504, 4096], P('col', 'row'), may hold values from -0.078125 to 0.078125
- probe_gate: int32 [4096, 5504], P('row', 'col'), may hold values from 0 to 1
- probe_up: int32 [4096, 5504], P('row', 'col'), may hold values from 0 to 1
- probe_down: int32 [5504, 4096], P('col', 'row'), may hold values from 0 to 1
- first_gate: float32 [4096, 5504], P('row', 'col'), may hold values from -1.8 to 1.8
- first_up: float32 [4096, 5504], P('row', 'col'), may hold values from -1.8 to 1.8
- first_down: float32 [5504, 4096], P('col', 'row'), may hold values from -1.8 to 1.8
- second_gate: float32 [4096, 5504], P('row', 'col'), may hold values from 0.01 to 0.2
- second_up: float32 [4096, 5504], P('row', 'col'), may hold values from 0.01 to 0.2
- second_down: float32 [5504, 4096], P('col', 'row'), may hold values from 0.01 to 0.2
Outputs:
- new_first_gate: float32 [4096, 5504], P('row', 'col')
- new_first_up: float32 [4096, 5504], P('row', 'col')
- new_first_down: float32 [5504, 4096], P('col', 'row')
- new_second_gate: float32 [4096, 5504], P('row', 'col')
- new_second_up: float32 [4096, 5504], P('row', 'col')
- new_second_down: float32 [5504, 4096], P('col', 'row')
- update_gate: float32 [4096, 5504], P('row', 'col')
- update_up: float32 [4096, 5504], P('row', 'col')
- update_down: float32 [5504, 4096], P('col', 'row')
Inputs may be any that keep to these rules, and one draw needn't show every extreme that they name: `probe_gate`: probe bits; the probe is 2 p - 1. `probe_up`: probe bits; the probe is 2 p - 1. `probe_down`: probe bits; the probe is 2 p - 1.
All inputs are finite; a program needn't handle non-finite values.
Results may differ from a plain program's by a relative error of at most 0.038.
Values may be sent and summed in bfloat16 or wider, within the bound.
A program may use at most 128 MiB of HBM per device.

v0:
```python
import functools

import jax
import jax.numpy as jnp
from jax import lax
from jax.sharding import Mesh
from jax.sharding import PartitionSpec as P

D = 4096
FF = 5504
STEP = 10
COL = ("col_0", "col_1")
ROW = ("row_0", "row_1", "row_2")
ROW_COL = ("row_0", "row_1", "row_2", "col_0", "col_1")


def copy_for_each(shard, axis):
    length = lax.axis_size(axis)
    return lax.all_to_all(
        jnp.broadcast_to(shard[None], (length, *shard.shape)), axis, 0, 0, tiled=True
    )


def laid_out(parts, dim):
    parts = jnp.moveaxis(parts, 0, dim)
    dims = parts.shape
    return parts.reshape(*dims[:dim], dims[dim] * dims[dim + 1], *dims[dim + 2 :])


def collect(shard, axis, dim):
    parts = copy_for_each(shard, axis)
    return laid_out(parts, dim)


def split_up(shard, dim, length):
    dims = shard.shape
    parts = shard.reshape(*dims[:dim], length, dims[dim] // length, *dims[dim + 1 :])
    return jnp.moveaxis(parts, dim, 0)


def sent_and_summed(shard, axis, dim):
    length = lax.axis_size(axis)
    parts = lax.all_to_all(split_up(shard, dim, length), axis, 0, 0, tiled=True)
    return jnp.sum(parts.astype(jnp.float32), axis=0)


def over_axes(shard, axes):
    return functools.reduce(lax.psum, axes, shard)


def activation(pre):
    sig = jax.nn.sigmoid(pre)
    act = pre * sig
    slope = sig * (1.0 + pre * (1.0 - sig))
    bend = sig * (1.0 - sig) * (2.0 + pre * (1.0 - 2.0 * sig))
    return (act, slope, bend)


def block_mean(values):
    height, breadth = values.shape
    means = values.reshape(height // 4, 4, breadth // 4, 4).mean(axis=(1, 3))
    return jnp.broadcast_to(means[:, None, :, None], (height // 4, 4, breadth // 4, 4)).reshape(
        height, breadth
    )


def matmul(left, right):
    return jnp.dot(left, right, preferred_element_type=jnp.float32)


def inner_first(left, right):
    return lax.dot_general(
        left, right, (((0,), (0,)), ((), ())), preferred_element_type=jnp.float32
    )


def inner_last(left, right):
    return lax.dot_general(
        left, right, (((1,), (1,)), ((), ())), preferred_element_type=jnp.float32
    )


def body(
    tokens,
    target,
    gate_weight,
    up_weight,
    down_weight,
    probe_gate,
    probe_up,
    probe_down,
    first_gate,
    first_up,
    first_down,
    second_gate,
    second_up,
    second_down,
):
    whole = collect(tokens, COL, 0)
    sign_gate = (2 * probe_gate - 1).astype(jnp.bfloat16)
    sign_up = (2 * probe_up - 1).astype(jnp.bfloat16)
    sign_down = (2 * probe_down - 1).astype(jnp.bfloat16)
    width = gate_weight.shape[1]

    def projector(matrices):
        return jnp.concatenate([matmul(whole, matrix) for matrix in matrices], axis=1)

    sums = sent_and_summed(projector((gate_weight, up_weight)).astype(jnp.bfloat16), ROW, 0)
    pre_gate = sums[:, :width]
    pre_up = sums[:, width:]
    act, slope, bend = activation(pre_gate)
    hidden = (act * pre_up).astype(jnp.bfloat16)
    moved = sent_and_summed(projector((sign_gate, sign_up)).astype(jnp.bfloat16), ROW, 0)
    dot_gate = moved[:, :width]
    dot_up = moved[:, width:]
    hidden_dot = (slope * dot_gate * pre_up + act * dot_up).astype(jnp.bfloat16)
    both = jnp.concatenate([hidden, hidden_dot], axis=1)
    piece = lax.all_gather(both, ROW, axis=0, tiled=True)
    plain = piece[:, :width]
    tangent = piece[:, width:]
    value = matmul(plain, down_weight)
    along = matmul(tangent, down_weight) + matmul(plain, sign_down)
    terms = jnp.concatenate([value, along], axis=1)
    outputs = sent_and_summed(terms.astype(jnp.bfloat16), COL, 0)
    feats_here = down_weight.shape[1]
    resid = outputs[:, :feats_here] - target.astype(jnp.float32)
    errors = jnp.concatenate(
        [resid.astype(jnp.bfloat16), outputs[:, feats_here:].astype(jnp.bfloat16)], axis=1
    )
    err_all = lax.all_gather(errors, COL, axis=0, tiled=True)
    block = err_all
    err = block[:, :feats_here]
    err_dot = block[:, feats_here:]
    plain = inner_last(err, down_weight)
    along = inner_last(err_dot, down_weight) + inner_last(err, sign_down)
    back = sent_and_summed(jnp.concatenate([plain, along], axis=1).astype(jnp.bfloat16), ROW, 0)
    d_hidden = back[:, :width]
    d_hidden_dot = back[:, width:]
    block = err_all
    piece = lax.all_gather(both, ROW, axis=0, tiled=True)
    plain = piece[:, :width]
    tangent = piece[:, width:]
    err = block[:, :feats_here]
    err_dot = block[:, feats_here:]
    grad_part = inner_first(plain, err)
    hess_part = inner_first(tangent, err) + inner_first(plain, err_dot)
    d_gate = (d_hidden * pre_up * slope).astype(jnp.bfloat16)
    d_up = (d_hidden * act).astype(jnp.bfloat16)
    dd_gate = (
        d_hidden_dot * pre_up * slope
        + d_hidden * dot_up * slope
        + d_hidden * pre_up * bend * dot_gate
    ).astype(jnp.bfloat16)
    dd_up = (d_hidden_dot * act + d_hidden * slope * dot_gate).astype(jnp.bfloat16)
    stacked = jnp.concatenate([d_gate, d_up, dd_gate, dd_up], axis=1)
    block = whole
    grads = inner_first(block, lax.all_gather(stacked, ROW, axis=0, tiled=True))
    grad_gate = grads[:, :width]
    grad_up = grads[:, width : 2 * width]
    hess_gate = grads[:, 2 * width : 3 * width]
    hess_up = grads[:, 3 * width :]
    curv_gate = block_mean(jnp.abs(sign_gate.astype(jnp.float32) * hess_gate))
    curv_up = block_mean(jnp.abs(sign_up.astype(jnp.float32) * hess_up))
    curv_down = block_mean(jnp.abs(sign_down.astype(jnp.float32) * hess_part))
    local_grad = (
        jnp.sum(grad_gate * grad_gate) + jnp.sum(grad_up * grad_up) + jnp.sum(grad_part * grad_part)
    )
    local_curv = (
        jnp.sum(curv_gate * curv_gate) + jnp.sum(curv_up * curv_up) + jnp.sum(curv_down * curv_down)
    )
    total_grad, total_curv = (over_axes(local_grad, ROW_COL), over_axes(local_curv, ROW_COL))
    count = 3.0 * D * FF
    rms_grad = jnp.sqrt(total_grad / count + 1e-06)
    rms_curv = jnp.sqrt(total_curv / count + 1e-06)
    fix_first = 1.0 - 0.9**STEP
    fix_second = 1.0 - 0.95**STEP
    firsts = []
    seconds = []
    updates = []
    for grad, curv, first, second in (
        (grad_gate, curv_gate, first_gate, second_gate),
        (grad_up, curv_up, first_up, second_up),
        (grad_part, curv_down, first_down, second_down),
    ):
        new_first = 0.9 * first + 0.1 * (grad / rms_grad)
        scaled = curv / rms_curv
        new_second = 0.95 * second + 0.05 * (scaled * scaled)
        firsts.append(new_first)
        seconds.append(new_second)
        updates.append(new_first / fix_first / (jnp.sqrt(new_second / fix_second) + 1e-08))
    return (
        firsts[0],
        firsts[1],
        firsts[2],
        seconds[0],
        seconds[1],
        seconds[2],
        updates[0],
        updates[1],
        updates[2],
    )


def solution(mesh):
    torus = Mesh(mesh.devices.reshape(4, 2, 2, 4, 4), ("row_0", "row_1", "row_2", "col_0", "col_1"))
    in_specs = (
        P(COL, ROW),
        P(COL, ROW),
        P(ROW, COL),
        P(ROW, COL),
        P(COL, ROW),
        P(ROW, COL),
        P(ROW, COL),
        P(COL, ROW),
        P(ROW, COL),
        P(ROW, COL),
        P(COL, ROW),
        P(ROW, COL),
        P(ROW, COL),
        P(COL, ROW),
    )
    out_specs = (
        P(ROW, COL),
        P(ROW, COL),
        P(COL, ROW),
        P(ROW, COL),
        P(ROW, COL),
        P(COL, ROW),
        P(ROW, COL),
        P(ROW, COL),
        P(COL, ROW),
    )
    return jax.shard_map(body, mesh=torus, in_specs=in_specs, out_specs=out_specs, check_vma=False)
```

profile of v0, /device:TPU:32, one launch (start us, length us, event | category | flops | bytes accessed | tf_op | source)
XLA Modules:
  0.0 556.4 jit_solution(3519608438580299076)
XLA Ops:
  8.2 38.9 %all_to_all.25 = bf16[16,128,256]{2,1,0:T(8,128)(2,1)S(1)} all-to-all(bf16[16,128,256]{2,1,0:T(8,128)(2,1)S(1)} %broadcast_in_dim.14), channel_id=1, replica_groups=mesh['row_0'=4,'row_1'=2,'row_2'=2,'col_0'=4,'col_1'=4] {'col_0','col_1'}, dimensions={0} | all-to-all | bytes 2097152 | tf_op jit(solution)/shard_map/all_to_all | solution.py:19
  50.5 5.9 %all-to-all-start.2 = ((bf16[16,128,688]{1,2,0:T(8,128)(2,1)}), bf16[16,128,688]{1,2,0:T(8,128)(2,1)}, u32[]{:S(2)}, u32[]{:S(2)}) async-start(bf16[16,128,688]{1,2,0:T(8,128)(2,1)} %pad_maximum_fusion.1), calls=%async_computation.2 | async-start | bytes 5636096 | tf_op jit(solution)/shard_map/all_to_all | solution.py:43
  59.4 31.5 %all-to-all-done.2 = bf16[16,128,688]{1,2,0:T(8,128)(2,1)} async-done(((bf16[16,128,688]{1,2,0:T(8,128)(2,1)}), bf16[16,128,688]{1,2,0:T(8,128)(2,1)}, u32[]{:S(2)}, u32[]{:S(2)}) %all-to-all-start.2) | async-done | bytes 2818080 | tf_op jit(solution)/shard_map/all_to_all | solution.py:43
  90.9 5.5 all-to-all-start.1
  98.7 32.2 %all-to-all-done.1 = bf16[16,128,688]{1,2,0:T(8,128)(2,1)} async-done(((bf16[16,128,688]{1,2,0:T(8,128)(2,1)}), bf16[16,128,688]{1,2,0:T(8,128)(2,1)}, u32[]{:S(2)}, u32[]{:S(2)}) %all-to-all-start.1) | async-done | bytes 2818080 | tf_op jit(solution)/shard_map/all_to_all | solution.py:43
  134.7 37.5 %all-gather.4.cloned.1.call-done = bf16[2048,688]{0,1:T(8,128)(2,1)} async-done(((bf16[128,688]{0,1:T(8,128)(2,1)}), bf16[2048,688]{0,1:T(8,128)(2,1)}) %all-gather.4.cloned.1.call-update) | async-done | bytes 2818064 | tf_op jit(solution)/shard_map/all_gather | solution.py:118
  172.3 2.3 convolution_convert_fusion.3
  176.3 61.0 %all_to_all.26 = bf16[16,128,512]{2,1,0:T(8,128)(2,1)S(1)} all-to-all(bf16[16,128,512]{2,1,0:T(8,128)(2,1)S(1)} %pad_maximum_fusion.3), channel_id=1, replica_groups=mesh['row_0'=4,'row_1'=2,'row_2'=2,'col_0'=4,'col_1'=4] {'col_0','col_1'}, dimensions={0} | all-to-all | bytes 4194304 | tf_op jit(solution)/shard_map/all_to_all | solution.py:43
  238.4 54.1 %all-gather.6.cloned.1.call-done = bf16[2048,512]{1,0:T(8,128)(2,1)} async-done(((bf16[128,512]{1,0:T(8,128)(2,1)}), bf16[2048,512]{1,0:T(8,128)(2,1)}) %all-gather.6.cloned.1.call-update) | async-done | bytes 2097168 | tf_op jit(solution)/shard_map/all_gather | solution.py:130
  296.5 40.0 %all_to_all.27 = bf16[16,128,688]{1,2,0:T(8,128)(2,1)S(1)} all-to-all(bf16[16,128,688]{1,2,0:T(8,128)(2,1)S(1)} %pad_maximum_fusion.2), channel_id=1, replica_groups=mesh['row_0'=4,'row_1'=2,'row_2'=2,'col_0'=4,'col_1'=4] {'row_0','row_1'..., dimensions={0} | all-to-all | bytes 5636096 | tf_op jit(solution)/shard_map/all_to_all | solution.py:43
  340.8 2.3 fusion.16
  343.1 13.4 %reshape.83 = f32[86,4,64,4]{3,2,1,0:T(8,128)} reshape(f32[344,256]{1,0:T(8,128)} %fusion.16) | data formatting | bytes 704512 | tf_op jit(solution)/shard_map/reshape | solution.py:61
  356.5 5.2 reduce_sum.128
  362.5 3.3 multiply_reduce_fusion
  365.8 22.9 %all-gather.8.cloned.1.call-done = bf16[2048,1376]{0,1:T(8,128)(2,1)} async-done(((bf16[128,1376]{0,1:T(8,128)(2,1)}), bf16[2048,1376]{0,1:T(8,128)(2,1)}) %all-gather.8.cloned.1.call-update) | async-done | bytes 5636112 | tf_op jit(solution)/shard_map/all_gather | solution.py:157
  388.7 4.3 convolution_bitcast_fusion
  393.7 16.0 %reshape.82 = f32[64,4,86,4]{1,0,3,2:T(8,128)} reshape(f32[256,344]{0,1:T(8,128)S(1)} %get-tuple-element.33) | data formatting | bytes 704512 | tf_op jit(solution)/shard_map/reshape | solution.py:61
  409.7 5.0 reduce_sum.126
  415.5 27.2 %reshape.81 = f32[64,4,86,4]{1,0,3,2:T(8,128)} reshape(f32[256,344]{0,1:T(8,128)S(1)} %get-tuple-element.34) | data formatting | bytes 704512 | tf_op jit(solution)/shard_map/reshape | solution.py:61
  442.7 5.0 reduce_sum.124
  452.5 8.9 %all-reduce.2 = (f32[]{:T(128)}, f32[]{:T(128)}) all-reduce(f32[]{:T(128)S(6)} %add.111, f32[]{:T(128)S(6)} %add.118), channel_id=1, replica_groups=mesh['row_0'=4,'row_1'=2,'row_2'=2,'col_0'=4,'col_1'=4] {'row_0'}, use_global_device_ids=true, to_apply=%region_7.0 | all-reduce | flops 2 | bytes 16 | tf_op jit(solution)/shard_map/psum | solution.py:48
  461.4 5.7 %all-reduce.4 = (f32[]{:T(128)}, f32[]{:T(128)}) all-reduce(f32[]{:T(128)} %get-tuple-element.15, f32[]{:T(128)} %get-tuple-element.16), channel_id=1, replica_groups=mesh['row_0'=4,'row_1'=2,'row_2'=2,'col_0'=4,'col_1'=4] {'row_1'}, use_global_device_ids=true, to_apply=%region_8.0 | all-reduce | flops 2 | bytes 16 | tf_op jit(solution)/shard_map/psum | solution.py:48
  467.1 3.1 all-reduce.3
  470.2 13.0 %all-reduce.1 = (f32[]{:T(128)}, f32[]{:T(128)}) all-reduce(f32[]{:T(128)} %get-tuple-element.17, f32[]{:T(128)} %get-tuple-element.18), channel_id=1, replica_groups=mesh['row_0'=4,'row_1'=2,'row_2'=2,'col_0'=4,'col_1'=4] {'col_0'}, use_global_device_ids=true, to_apply=%region_10.0 | all-reduce | flops 2 | bytes 16 | tf_op jit(solution)/shard_map/psum | solution.py:48
  483.1 11.1 %all-reduce = (f32[]{:T(128)}, f32[]{:T(128)}) all-reduce(f32[]{:T(128)} %get-tuple-element.13, f32[]{:T(128)} %get-tuple-element.14), channel_id=1, replica_groups=mesh['row_0'=4,'row_1'=2,'row_2'=2,'col_0'=4,'col_1'=4] {'col_1'}, use_global_device_ids=true, to_apply=%region_11.0 | all-reduce | flops 2 | bytes 16 | tf_op jit(solution)/shard_map/psum | solution.py:48
  495.7 5.7 %broadcast_in_dim.34 = f32[64,4,86,4]{1,0,3,2:T(8,128)} broadcast(f32[64,86]{0,1:T(8,128)S(1)} %multiply_multiply_fusion.2), dimensions={0,2} | broadcast | bytes 374272 | tf_op jit(solution)/shard_map/broadcast_in_dim | solution.py:62
  501.4 10.5 %mul.237 = f32[256,344]{0,1:T(8,128)S(1)} reshape(f32[64,4,86,4]{1,0,3,2:T(8,128)} %broadcast_in_dim.34) | data formatting | bytes 704512 | tf_op jit(solution)/shard_map/mul | solution.py:187
  511.9 5.7 %broadcast_in_dim.36 = f32[86,4,64,4]{3,2,1,0:T(8,128)} broadcast(f32[86,64]{1,0:T(8,128)S(1)} %multiply_multiply_fusion), dimensions={0,2} | broadcast | bytes 374272 | tf_op jit(solution)/shard_map/broadcast_in_dim | solution.py:62
  517.7 10.5 %mul.247 = f32[344,256]{1,0:T(8,128)S(1)} reshape(f32[86,4,64,4]{3,2,1,0:T(8,128)} %broadcast_in_dim.36) | data formatting | bytes 704512 | tf_op jit(solution)/shard_map/mul | solution.py:187
  528.2 5.7 %broadcast_in_dim.35 = f32[64,4,86,4]{1,0,3,2:T(8,128)} broadcast(f32[64,86]{0,1:T(8,128)S(1)} %multiply_multiply_fusion.1), dimensions={0,2} | broadcast | bytes 374272 | tf_op jit(solution)/shard_map/broadcast_in_dim | solution.py:62
  533.9 10.6 %mul.241 = f32[256,344]{0,1:T(8,128)S(1)} reshape(f32[64,4,86,4]{1,0,3,2:T(8,128)} %broadcast_in_dim.35) | data formatting | bytes 704512 | tf_op jit(solution)/shard_map/mul | solution.py:187
  546.8 2.9 add_divide_fusion.1
  (87 shorter events, 29.9 us)
Async XLA Ops:
  7.2 165.1 %copy-start = (bf16[344,256]{1,0:T(8,128)(2,1)S(1)}, bf16[344,256]{1,0:T(8,128)(2,1)}, u32[]{:S(2)}) copy-start(bf16[344,256]{1,0:T(8,128)(2,1)} %param.18) | copy-start | bytes 528388
  7.2 39.9 %copy-start.9 = (s32[256,344]{0,1:T(8,128)S(1)}, s32[256,344]{0,1:T(8,128)}, u32[]{:S(2)}) copy-start(s32[256,344]{0,1:T(8,128)} %param.20) | copy-start | bytes 1056772
  7.2 40.5 %copy-start.11 = (s32[256,344]{0,1:T(8,128)S(1)}, s32[256,344]{0,1:T(8,128)}, u32[]{:S(2)}) copy-start(s32[256,344]{0,1:T(8,128)} %param.19) | copy-start | bytes 1056772
  50.5 5.9 %copy-start.16 = (bf16[256,344]{0,1:T(8,128)(2,1)S(1)}, bf16[256,344]{0,1:T(8,128)(2,1)}, u32[]{:S(2)}) copy-start(bf16[256,344]{0,1:T(8,128)(2,1)} %param.17) | copy-start | bytes 528388
  50.5 6.5 %copy-start.17 = (bf16[256,344]{0,1:T(8,128)(2,1)S(1)}, bf16[256,344]{0,1:T(8,128)(2,1)}, u32[]{:S(2)}) copy-start(bf16[256,344]{0,1:T(8,128)(2,1)} %param.16) | copy-start | bytes 528388
  50.5 40.3 %all-to-all-start.2 = ((bf16[16,128,688]{1,2,0:T(8,128)(2,1)}), bf16[16,128,688]{1,2,0:T(8,128)(2,1)}, u32[]{:S(2)}, u32[]{:S(2)}) async-start(bf16[16,128,688]{1,2,0:T(8,128)(2,1)} %pad_maximum_fusion.1), calls=%async_computation.2 | async-start | bytes 5636096 | tf_op jit(solution)/shard_map/all_to_all | solution.py:43
  90.9 40.0 %all-to-all-start.1 = ((bf16[16,128,688]{1,2,0:T(8,128)(2,1)}), bf16[16,128,688]{1,2,0:T(8,128)(2,1)}, u32[]{:S(2)}, u32[]{:S(2)}) async-start(bf16[16,128,688]{1,2,0:T(8,128)(2,1)} %pad_maximum_fusion), calls=%async_computation.1 | async-start | bytes 5636096 | tf_op jit(solution)/shard_map/all_to_all | solution.py:43
  96.4 75.8 %all-gather.4.cloned.1.call-start = ((), (), s32[]{:S(2)}) async-start(), calls=%async_computation.5 | async-start | bytes 2994176 | tf_op jit(solution)/shard_map/all_gather | solution.py:118
  98.7 75.9 %copy-start.3 = (f32[128,688]{0,1:T(8,128)}, f32[128,688]{0,1:T(8,128)S(1)}, u32[]{:S(2)}) copy-start(f32[128,688]{0,1:T(8,128)S(1)} %convert_reduce_fusion.1) | copy-start | bytes 1056772
  133.1 0.7 copy-start.5
  134.7 40.7 %copy-start.13 = (s32[344,256]{1,0:T(8,128)S(1)}, s32[344,256]{1,0:T(8,128)}, u32[]{:S(2)}) copy-start(s32[344,256]{1,0:T(8,128)} %param.21) | copy-start | bytes 1056772
  134.7 157.9 %all-gather.6.cloned.1.call-start = ((), (), s32[]{:S(2)}) async-start(), calls=%async_computation.6 | async-start | bytes 2228224 | tf_op jit(solution)/shard_map/all_gather | solution.py:130
  172.3 2.3 copy-start.7
  176.3 61.3 %copy-start.18 = (bf16[128,256]{1,0:T(8,128)(2,1)S(1)}, bf16[128,256]{1,0:T(8,128)(2,1)}, u32[]{:S(2)}) copy-start(bf16[128,256]{1,0:T(8,128)(2,1)} %param.15) | copy-start | bytes 196612
  238.4 150.3 %all-gather.8.cloned.1.call-start = ((), (), s32[]{:S(2)}) async-start(), calls=%async_computation.7 | async-start | bytes 5988352 | tf_op jit(solution)/shard_map/all_gather | solution.py:157
  292.6 2.2 copy-start.2
  294.5 1.0 copy-start.14
  336.5 1.0 copy-start.4
  336.5 1.1 copy-start.6
  338.6 2.2 copy-start.8
  365.8 27.2 %copy-start.10 = (s32[256,344]{0,1:T(8,128)S(1)}, s32[256,344]{0,1:T(8,128)}, u32[]{:S(2)}) copy-start(s32[256,344]{0,1:T(8,128)} %param.20) | copy-start | bytes 1056772
  365.8 27.2 %copy-start.12 = (s32[256,344]{0,1:T(8,128)S(1)}, s32[256,344]{0,1:T(8,128)}, u32[]{:S(2)}) copy-start(s32[256,344]{0,1:T(8,128)} %param.19) | copy-start | bytes 1056772
  533.9 10.6 %copy-start.15 = (f32[344,256]{1,0:T(8,128)S(1)}, f32[344,256]{1,0:T(8,128)}, u32[]{:S(2)}) copy-start(f32[344,256]{1,0:T(8,128)} %param.27) | copy-start | bytes 1056772
  544.5 5.1 copy-start.1
Sparse Core Ops, SparseCore 0:
  134.8 37.4 all-gather.3
  238.5 54.0 all-gather.5
  338.7 49.9 all-gather.7
where the time goes:
time: 560 us; the launch traced here: 556 us
  blocking collectives  182 us (32%)
  waiting for transfers between devices  178 us (32%)
  local copies, waits for them, and re-layouts  109 us (19%)
  other arithmetic  34.8 us (6%)
  matrix products  21.1 us (4%)
  between operations  19.6 us (4%)
  starting transfers between devices  11.6 us (2%)
    all_to_all x2, blocking collectives, sent_and_summed(): parts = lax.all_to_all(split_up(shard, dim, length), axis, 0, 0, tiled=True)  101 us
    all_to_all x2, waiting for transfers between devices, sent_and_summed(): parts = lax.all_to_all(split_up(shard, dim, length), axis, 0, 0, tiled=True)  63.7 us
    reshape x3, local copies, waits for them, and re-layouts, block_mean(): means = values.reshape(height // 4, 4, breadth // 4, 4).mean(axis=(1, 3))  56.5 us
    all_gather x1, waiting for transfers between devices, body(): err_all = lax.all_gather(errors, COL, axis=0, tiled=True)  54.1 us
    psum x5, blocking collectives, over_axes(): return functools.reduce(lax.psum, axes, shard)  41.8 us
    all_to_all x1, blocking collectives, copy_for_each(): lax.all_to_all(jnp.broadcast_to(shard[None], (length, *shard.shape)), axi...  38.9 us
    all_gather x1, waiting for transfers between devices, body(): piece = lax.all_gather(both, ROW, axis=0, tiled=True)  37.5 us
    mul x3, local copies, waits for them, and re-layouts, body(): new_second = 0.95 * second + 0.05 * (scaled * scaled)  31.6 us
  transfers between devices with their start and end apart: 5, of which 5 were waited for; matrix products, arithmetic and copies ran while one was open for 6% of the time, Pallas kernels for 0%

commit v1 on v0

--- a/solution.py
+++ b/solution.py
@@ -3,6 +3,8 @@
 import jax
 import jax.numpy as jnp
 from jax import lax
+from jax.experimental import pallas as pl
+from jax.experimental.pallas import tpu as pltpu
 from jax.sharding import Mesh
 from jax.sharding import PartitionSpec as P
 
@@ -56,12 +58,43 @@
     return (act, slope, bend)
 
 
-def block_mean(values):
-    height, breadth = values.shape
-    means = values.reshape(height // 4, 4, breadth // 4, 4).mean(axis=(1, 3))
-    return jnp.broadcast_to(means[:, None, :, None], (height // 4, 4, breadth // 4, 4)).reshape(
-        height, breadth
-    )
+def block_ones(size):
+    rows = lax.broadcasted_iota(jnp.int32, (size, size), 0) >> 2
+    cols = lax.broadcasted_iota(jnp.int32, (size, size), 1) >> 2
+    return (rows == cols).astype(jnp.float32)
+
+
+def exact_dot(left, right):
+    return jnp.dot(
+        left, right, preferred_element_type=jnp.float32, precision=lax.Precision.HIGHEST
+    )
+
+
+def curvature(sign, hess):
+    height, breadth = hess.shape
+    down = exact_dot(block_ones(height), jnp.abs(sign * hess))
+    return exact_dot(down, block_ones(breadth)) * 0.0625
+
+
+def tail_kernel(*refs):
+    hess_refs, sign_refs, grad_refs, curv_refs, sums_ref = (
+        refs[0:3],
+        refs[3:6],
+        refs[6:9],
+        refs[9:12],
+        refs[12],
+    )
+    grad_sum = 0.0
+    curv_sum = 0.0
+    for hess_ref, sign_ref, grad_ref, curv_ref in zip(hess_refs, sign_refs, grad_refs, curv_refs):
+        sign = (2 * sign_ref[...] - 1).astype(jnp.float32)
+        curv = curvature(sign, hess_ref[...])
+        curv_ref[...] = curv
+        grad = grad_ref[...]
+        grad_sum = grad_sum + jnp.sum(grad * grad, axis=(0, 1), keepdims=True)
+        curv_sum = curv_sum + jnp.sum(curv * curv, axis=(0, 1), keepdims=True)
+    lane = lax.broadcasted_iota(jnp.int32, (1, 128), 1)
+    sums_ref[...] = jnp.where(lane == 0, grad_sum, jnp.where(lane == 1, curv_sum, 0.0))
 
 
 def matmul(left, right):
@@ -159,16 +192,16 @@
     grad_up = grads[:, width : 2 * width]
     hess_gate = grads[:, 2 * width : 3 * width]
     hess_up = grads[:, 3 * width :]
-    curv_gate = block_mean(jnp.abs(sign_gate.astype(jnp.float32) * hess_gate))
-    curv_up = block_mean(jnp.abs(sign_up.astype(jnp.float32) * hess_up))
-    curv_down = block_mean(jnp.abs(sign_down.astype(jnp.float32) * hess_part))
-    local_grad = (
-        jnp.sum(grad_gate * grad_gate) + jnp.sum(grad_up * grad_up) + jnp.sum(grad_part * grad_part)
-    )
-    local_curv = (
-        jnp.sum(curv_gate * curv_gate) + jnp.sum(curv_up * curv_up) + jnp.sum(curv_down * curv_down)
-    )
-    total_grad, total_curv = (over_axes(local_grad, ROW_COL), over_axes(local_curv, ROW_COL))
+    shapes = [jax.ShapeDtypeStruct(probe.shape, jnp.float32) for probe in (probe_gate, probe_up, probe_down)]
+    curv_gate, curv_up, curv_down, sums = pl.pallas_call(
+        tail_kernel,
+        out_shape=(*shapes, jax.ShapeDtypeStruct((1, 128), jnp.float32)),
+        in_specs=[pl.BlockSpec(memory_space=pltpu.VMEM)] * 9,
+        out_specs=[pl.BlockSpec(memory_space=pltpu.VMEM)] * 4,
+        compiler_params=pltpu.CompilerParams(vmem_limit_bytes=40 * 1024 * 1024),
+    )(hess_gate, hess_up, hess_part, probe_gate, probe_up, probe_down, grad_gate, grad_up, grad_part)
+    totals = lax.psum(sums[0, :2], ROW_COL)
+    total_grad, total_curv = totals[0], totals[1]
     count = 3.0 * D * FF
     rms_grad = jnp.sqrt(total_grad / count + 1e-06)
     rms_curv = jnp.sqrt(total_curv / count + 1e-06)

time: 560 us -> 498 us (0.89)
  local copies, waits for them, and re-layouts: 109 us -> 18.6 us
  blocking collectives: 182 us -> 216 us
  other arithmetic: 34.8 us -> 15.7 us
  waiting for transfers between devices: 178 us -> 196 us
    reshape x3 -> x0, local copies, waits for them, and re-layouts: 56.5 us -> none  [block_mean(): means = values.reshape(height // 4, 4, breadth // 4, 4).mean(axis=(1, 3))]
    psum x5 -> x1, blocking collectives: 41.8 us -> 76.6 us  [body(): totals = lax.psum(sums[0, :2], ROW_COL)]
    mul x6 -> x0, local copies, waits for them, and re-layouts: 31.8 us -> none  [the longest x3 31.6 us: body(): new_second = 0.95 * second + 0.05 * (scaled * scaled)]
    all_gather x1, waiting for transfers between devices: 22.9 us -> 40.8 us  [body(): grads = inner_first(block, lax.all_gather(stacked, ROW, axis=0, tiled=True))]
    reduce_sum x6 -> x0, other arithmetic: 17.5 us -> none  [the longest x3 15.2 us: block_mean(): means = values.reshape(height // 4, 4, breadth // 4, 4).mean(axis=(1, 3))]
    broadcast_in_dim x3 -> x0, local copies, waits for them, and re-layouts: 17.2 us -> none  [block_mean(): jnp.broadcast_to(means[:, None, :, None], (height // 4, 4, breadth // 4, 4))]
    unnamed x38 -> x48, local copies, waits for them, and re-layouts: 1.77 us -> 15.6 us
  transfers between devices with their start and end apart: 5 -> 5, of which waited for: 5 -> 5; matrix products, arithmetic and copies ran while one was open for 6% -> 3% of each run, Pallas kernels for 0% -> 0%
where the time goes in v1:
time: 498 us; the launch traced here: 496 us
  blocking collectives  216 us (43%)
  waiting for transfers between devices  196 us (39%)
  local copies, waits for them, and re-layouts  18.6 us (4%)
  matrix products  18.6 us (4%)
  other arithmetic  15.7 us (3%)
  between operations  15.5 us (3%)
  starting transfers between devices  11.6 us (2%)
    all_to_all x2, blocking collectives, sent_and_summed(): parts = lax.all_to_all(split_up(shard, dim, length), axis, 0, 0, tiled=True)  101 us
    psum x1, blocking collectives, body(): totals = lax.psum(sums[0, :2], ROW_COL)  76.6 us
    all_to_all x2, waiting for transfers between devices, sent_and_summed(): parts = lax.all_to_all(split_up(shard, dim, length), axis, 0, 0, tiled=True)  63.4 us
    all_gather x1, waiting for transfers between devices, body(): err_all = lax.all_gather(errors, COL, axis=0, tiled=True)  54 us
    all_gather x1, waiting for transfers between devices, body(): grads = inner_first(block, lax.all_gather(stacked, ROW, axis=0, tiled=True))  40.8 us
    all_to_all x1, blocking collectives, copy_for_each(): lax.all_to_all(jnp.broadcast_to(shard[None], (length, *shard.shape)), axi...  39 us
    all_gather x1, waiting for transfers between devices, body(): piece = lax.all_gather(both, ROW, axis=0, tiled=True)  37.5 us
    unnamed x48, local copies, waits for them, and re-layouts  15.6 us
  transfers between devices with their start and end apart: 5, of which 5 were waited for; matrix products, arithmetic and copies ran while one was open for 3% of the time, Pallas kernels for 0%

profile of v1, /device:TPU:32, one launch (start us, length us, event | category | flops | bytes accessed | tf_op | source)
XLA Modules:
  0.0 496.3 jit_solution(1776808168266568314)
XLA Ops:
  7.2 1.0 broadcast_in_dim.2
  8.2 39.0 %all_to_all.25 = bf16[16,128,256]{2,1,0:T(8,128)(2,1)S(1)} all-to-all(bf16[16,128,256]{2,1,0:T(8,128)(2,1)S(1)} %broadcast_in_dim.2), channel_id=1, replica_groups=mesh['row_0'=4,'row_1'=2,'row_2'=2,'col_0'=4,'col_1'=4] {'col_0','col_1'}, dimensions={0} | all-to-all | bytes 2097152 | tf_op jit(solution)/shard_map/all_to_all | solution.py:21
  48.9 1.8 pad_maximum_fusion.1
  50.7 5.9 %all-to-all-start.2 = ((bf16[16,128,688]{1,2,0:T(8,128)(2,1)}), bf16[16,128,688]{1,2,0:T(8,128)(2,1)}, u32[]{:S(2)}, u32[]{:S(2)}) async-start(bf16[16,128,688]{1,2,0:T(8,128)(2,1)} %pad_maximum_fusion.1), calls=%async_computation.2 | async-start | bytes 5636096 | tf_op jit(solution)/shard_map/all_to_all | solution.py:45
  58.1 1.8 pad_maximum_fusion
  59.9 31.2 %all-to-all-done.2 = bf16[16,128,688]{1,2,0:T(8,128)(2,1)} async-done(((bf16[16,128,688]{1,2,0:T(8,128)(2,1)}), bf16[16,128,688]{1,2,0:T(8,128)(2,1)}, u32[]{:S(2)}, u32[]{:S(2)}) %all-to-all-start.2) | async-done | bytes 2818080 | tf_op jit(solution)/shard_map/all_to_all | solution.py:45
  91.0 5.5 %all-to-all-start.1 = ((bf16[16,128,688]{1,2,0:T(8,128)(2,1)}), bf16[16,128,688]{1,2,0:T(8,128)(2,1)}, u32[]{:S(2)}, u32[]{:S(2)}) async-start(bf16[16,128,688]{1,2,0:T(8,128)(2,1)} %pad_maximum_fusion), calls=%async_computation.1 | async-start | bytes 5636096 | tf_op jit(solution)/shard_map/all_to_all | solution.py:45
  96.6 2.2 convert_reduce_fusion.1
  98.8 32.2 %all-to-all-done.1 = bf16[16,128,688]{1,2,0:T(8,128)(2,1)} async-done(((bf16[16,128,688]{1,2,0:T(8,128)(2,1)}), bf16[16,128,688]{1,2,0:T(8,128)(2,1)}, u32[]{:S(2)}, u32[]{:S(2)}) %all-to-all-start.1) | async-done | bytes 2818080 | tf_op jit(solution)/shard_map/all_to_all | solution.py:45
  131.0 2.2 convert_reduce_fusion.2
  134.1 37.5 %all-gather.4.cloned.1.call-done = bf16[2048,688]{0,1:T(8,128)(2,1)} async-done(((bf16[128,688]{0,1:T(8,128)(2,1)}), bf16[2048,688]{0,1:T(8,128)(2,1)}) %all-gather.4.cloned.1.call-update) | async-done | bytes 2818064 | tf_op jit(solution)/shard_map/all_gather | solution.py:151
  171.7 2.3 fusion.8
  175.9 61.0 %all_to_all.26 = bf16[16,128,512]{2,1,0:T(8,128)(2,1)S(1)} all-to-all(bf16[16,128,512]{2,1,0:T(8,128)(2,1)S(1)} %pad_maximum_fusion.3), channel_id=1, replica_groups=mesh['row_0'=4,'row_1'=2,'row_2'=2,'col_0'=4,'col_1'=4] {'col_0','col_1'}, dimensions={0} | all-to-all | bytes 4194304 | tf_op jit(solution)/shard_map/all_to_all | solution.py:45
  238.5 54.0 %all-gather.6.cloned.1.call-done = bf16[2048,512]{1,0:T(8,128)(2,1)} async-done(((bf16[128,512]{1,0:T(8,128)(2,1)}), bf16[2048,512]{1,0:T(8,128)(2,1)}) %all-gather.6.cloned.1.call-update) | async-done | bytes 2097168 | tf_op jit(solution)/shard_map/all_gather | solution.py:163
  292.6 1.9 fusion.15
  296.4 39.8 %all_to_all.27 = bf16[16,128,688]{1,2,0:T(8,128)(2,1)S(1)} all-to-all(bf16[16,128,688]{1,2,0:T(8,128)(2,1)S(1)} %pad_maximum_fusion.2), channel_id=1, replica_groups=mesh['row_0'=4,'row_1'=2,'row_2'=2,'col_0'=4,'col_1'=4] {'row_0','row_1'..., dimensions={0} | all-to-all | bytes 5636096 | tf_op jit(solution)/shard_map/all_to_all | solution.py:45
  338.0 0.9 copy.36
  338.9 0.9 copy.46
  339.8 1.9 copy.47
  341.7 2.3 fusion.17.refs_8_
  344.1 2.1 fusion.13
  346.8 40.8 %all-gather.8.cloned.1.call-done = bf16[2048,1376]{0,1:T(8,128)(2,1)} async-done(((bf16[128,1376]{0,1:T(8,128)(2,1)}), bf16[2048,1376]{0,1:T(8,128)(2,1)}) %all-gather.8.cloned.1.call-update) | async-done | bytes 5636112 | tf_op jit(solution)/shard_map/all_gather | solution.py:190
  387.6 4.4 convolution_bitcast_fusion
  393.2 4.2 shard_map.205
  397.4 1.1 copy.48
  398.6 76.6 %psum.7 = f32[2]{0:T(128)S(1)} all-reduce(f32[2]{0:T(128)S(1)} %slice_bitcast_fusion), channel_id=1, replica_groups=mesh['row_0'=4,'row_1'=2,'row_2'=2,'col_0'=4,'col_1'=4] {'row_0','row_1'..., use_global_device_ids=true, to_apply=%region_4.0 | all-reduce | flops 2 | bytes 16 | tf_op jit(solution)/shard_map/psum | solution.py:203
  477.2 3.0 add_divide_fusion
  480.2 2.0 copy.49
  482.2 1.9 copy.50
  484.1 1.9 copy.51
  486.0 0.9 copy.52
  488.6 1.1 add_divide_fusion.2
  (72 shorter events, 15.3 us)
Async XLA Ops:
  7.2 164.5 %copy-start = (bf16[344,256]{1,0:T(8,128)(2,1)S(1)}, bf16[344,256]{1,0:T(8,128)(2,1)}, u32[]{:S(2)}) copy-start(bf16[344,256]{1,0:T(8,128)(2,1)} %param.18) | copy-start | bytes 528388
  7.2 40.0 %copy-start.9 = (s32[256,344]{0,1:T(8,128)S(1)}, s32[256,344]{0,1:T(8,128)}, u32[]{:S(2)}) copy-start(s32[256,344]{0,1:T(8,128)} %param.19) | copy-start | bytes 1056772
  8.2 39.6 %copy-start.10 = (s32[256,344]{0,1:T(8,128)S(1)}, s32[256,344]{0,1:T(8,128)}, u32[]{:S(2)}) copy-start(s32[256,344]{0,1:T(8,128)} %param.20) | copy-start | bytes 1056772
  50.7 5.9 %copy-start.15 = (bf16[256,344]{0,1:T(8,128)(2,1)S(1)}, bf16[256,344]{0,1:T(8,128)(2,1)}, u32[]{:S(2)}) copy-start(bf16[256,344]{0,1:T(8,128)(2,1)} %param.17) | copy-start | bytes 528388
  50.7 40.3 %all-to-all-start.2 = ((bf16[16,128,688]{1,2,0:T(8,128)(2,1)}), bf16[16,128,688]{1,2,0:T(8,128)(2,1)}, u32[]{:S(2)}, u32[]{:S(2)}) async-start(bf16[16,128,688]{1,2,0:T(8,128)(2,1)} %pad_maximum_fusion.1), calls=%async_computation.2 | async-start | bytes 5636096 | tf_op jit(solution)/shard_map/all_to_all | solution.py:45
  56.6 0.9 copy-start.16
  91.0 40.0 %all-to-all-start.1 = ((bf16[16,128,688]{1,2,0:T(8,128)(2,1)}), bf16[16,128,688]{1,2,0:T(8,128)(2,1)}, u32[]{:S(2)}, u32[]{:S(2)}) async-start(bf16[16,128,688]{1,2,0:T(8,128)(2,1)} %pad_maximum_fusion), calls=%async_computation.1 | async-start | bytes 5636096 | tf_op jit(solution)/shard_map/all_to_all | solution.py:45
  96.6 75.1 %all-gather.4.cloned.1.call-start = ((), (), s32[]{:S(2)}) async-start(), calls=%async_computation.5 | async-start | bytes 2994176 | tf_op jit(solution)/shard_map/all_gather | solution.py:151
  134.1 158.5 %all-gather.6.cloned.1.call-start = ((), (), s32[]{:S(2)}) async-start(), calls=%async_computation.6 | async-start | bytes 2228224 | tf_op jit(solution)/shard_map/all_gather | solution.py:163
  171.7 2.3 copy-start.6
  174.0 1.0 copy-start.2
  236.9 0.8 copy-start.17
  238.5 149.1 %all-gather.8.cloned.1.call-start = ((), (), s32[]{:S(2)}) async-start(), calls=%async_computation.7 | async-start | bytes 5988352 | tf_op jit(solution)/shard_map/all_gather | solution.py:190
  292.6 1.9 copy-start.3
  336.8 1.2 copy-start.13
  336.8 2.1 copy-start.14
  341.7 2.3 copy-start.4
  344.0 2.2 copy-start.7
  392.1 1.1 copy-start.5
  480.2 5.8 %copy-start.8 = (f32[256,344]{1,0:T(8,128)S(1)}, f32[256,344]{1,0:T(8,128)}, u32[]{:S(2)}) copy-start(f32[256,344]{1,0:T(8,128)} %get-tuple-element.39) | copy-start | bytes 1056772
  480.2 8.4 %copy-start.11 = (f32[344,256]{1,0:T(8,128)S(1)}, f32[344,256]{1,0:T(8,128)}, u32[]{:S(2)}) copy-start(f32[344,256]{1,0:T(8,128)} %param.27) | copy-start | bytes 1056772
  480.2 8.4 %copy-start.12 = (f32[344,256]{1,0:T(8,128)S(1)}, f32[344,256]{1,0:T(8,128)}, u32[]{:S(2)}) copy-start(f32[344,256]{1,0:T(8,128)} %param.24) | copy-start | bytes 1056772
  486.0 3.8 copy-start.1
Sparse Core Ops, SparseCore 0:
  134.2 37.4 all-gather.3
  238.6 53.9 all-gather.5
  337.7 49.8 all-gather.7

commit v2 on v0

v2 whole, which is shorter than its diff:
```python
import jax
import jax.numpy as jnp
from jax import lax
from jax.experimental import pallas as pl
from jax.experimental.pallas import tpu as pltpu
from jax.sharding import Mesh
from jax.sharding import PartitionSpec as P

D = 4096
FF = 5504
STEP = 10
COL = ("col_0", "col_1")
ROW = ("row_0", "row_1", "row_2")
RING = 4
UNITS = 344
PADDED = 352
FEATS = 256
HALF = 64
LANES = 128
STRIP = 32
MESH = pl.DeviceIdType.MESH
BF16 = jnp.bfloat16
F32 = jnp.float32

X_AXIS, Z_AXIS, CORE_AXIS = ROW
H_AXIS, Y_AXIS = COL


def dot_nn(left, right):
    return jnp.dot(left, right, preferred_element_type=F32)


def dot_nt(left, right):
    return lax.dot_general(left, right, (((1,), (1,)), ((), ())), preferred_element_type=F32)


def dot_tn(left, right):
    return lax.dot_general(left, right, (((0,), (0,)), ((), ())), preferred_element_type=F32)


def block_ones(size):
    rows = lax.broadcasted_iota(jnp.int32, (size, size), 0) >> 2
    cols = lax.broadcasted_iota(jnp.int32, (size, size), 1) >> 2
    return jnp.where(rows == cols, 1.0, 0.0).astype(BF16)


def two_terms(values):
    high = values.astype(BF16)
    low = (values - high.astype(F32)).astype(BF16)
    return high, low


def curvature(sign, hess):
    high, low = two_terms(jnp.abs(sign * hess))
    ones = block_ones(hess.shape[0])
    down = dot_nn(ones, high) + dot_nn(ones, low)
    high, low = two_terms(down)
    ones = block_ones(hess.shape[1])
    return (dot_nn(high, ones) + dot_nn(low, ones)) * 0.0625


class Copies:
    def __init__(self, send_sems, recv_sems):
        self.send_sems = send_sems
        self.recv_sems = recv_sems
        self.next = 0
        self.pending = []

    def slots(self, count):
        first = self.next
        self.next += count
        return first

    def copy(self, src, dst, slot, peer):
        return pltpu.make_async_remote_copy(
            src_ref=src,
            dst_ref=dst,
            send_sem=self.send_sems.at[slot],
            recv_sem=self.recv_sems.at[slot],
            device_id=peer,
            device_id_type=MESH,
        )

    def send(self, src, dst, slot, peer):
        self.copy(src, dst, slot, peer).start()

    def arrived(self, dst, slot, peer):
        self.copy(dst, dst, slot, peer).wait_recv()

    def sent(self, src, slot, peer):
        self.copy(src, src, slot, peer).wait_send()


def around(axis):
    here = lax.axis_index(axis)
    return here, lax.rem(here + 1, RING), lax.rem(here + 3, RING), lax.rem(here + 2, RING)


def add_strips(dst, terms):
    def strip(index, carry):
        rows = pl.ds(pl.multiple_of(index * STRIP, STRIP), STRIP)
        total = terms[0][rows, :].astype(F32)
        for term in terms[1:]:
            total = total + term[rows, :].astype(F32)
        dst[rows, :] = total.astype(dst.dtype)
        return carry

    lax.fori_loop(0, PADDED // STRIP, strip, 0)


def add_blocks(dst, terms):
    for part in range(2):
        total = terms[0][part].astype(F32)
        for term in terms[1:]:
            total = total + term[part].astype(F32)
        dst[part] = total.astype(dst.dtype)


class RingSum:
    def __init__(self, copies, axis, count, block, landed, add):
        self.copies, self.axis, self.block, self.landed, self.add = copies, axis, block, landed, add
        self.base = copies.slots(6 * count)
        self.count = count
        self.here, self.plus, self.minus, self.opposite = around(axis)

    def slot(self, kind, index):
        return self.base + kind * self.count + index

    def send(self, src, kind, index, peer):
        self.copies.send(src, self.landed(kind, index), self.slot(kind, index), {self.axis: peer})

    def wait(self, kind, index):
        ref = self.landed(kind, index)
        self.copies.arrived(ref, self.slot(kind, index), {self.axis: self.plus})

    def send_opposite(self, index):
        self.send(self.block(self.opposite, 0, index), 0, index, self.plus)
        self.send(self.block(self.opposite, 1, index), 1, index, self.minus)

    def send_plus(self, index):
        self.send(self.block(self.plus, 1, index), 3, index, self.plus)

    def send_minus(self, index):
        self.send(self.block(self.minus, 0, index), 4, index, self.minus)

    def forward(self, index):
        self.wait(0, index)
        ref = self.block(self.plus, 0, index)
        self.add(ref, (ref, self.landed(0, index)))
        self.send(ref, 2, index, self.plus)
        self.wait(1, index)
        ref = self.block(self.minus, 1, index)
        self.add(ref, (ref, self.landed(1, index)))
        self.send(ref, 5, index, self.minus)

    def wait_terms(self, index):
        for kind in (3, 4, 2, 5):
            self.wait(kind, index)

    def terms(self, half, index):
        return (
            self.block(self.here, half, index),
            self.landed(2 + half, index),
            self.landed(4 + half, index),
        )

    def drain(self, index):
        for kind in range(6):
            self.copies.sent(
                self.landed(kind, index), self.slot(kind, index), {self.axis: self.plus}
            )


class RowSum:
    def __init__(self, copies, count, blocks, landed, pair_sums, pair_landed):
        self.copies, self.count = copies, count
        self.ring = RingSum(
            copies,
            X_AXIS,
            count,
            lambda place, half, index: blocks.at[place, half, index],
            lambda kind, index: landed.at[kind, index],
            add_strips,
        )
        self.base = copies.slots(count)
        self.pair_sums, self.pair_landed = pair_sums, pair_landed
        self.z = lax.axis_index(Z_AXIS)
        self.other = 1 - self.z

    def pair(self, index):
        self.ring.wait_terms(index)
        add_strips(self.pair_sums.at[index], self.ring.terms(self.other, index))
        self.copies.send(
            self.pair_sums.at[index],
            self.pair_landed.at[index],
            self.base + index,
            {Z_AXIS: self.other},
        )

    def finish(self, dst, index):
        self.copies.arrived(self.pair_landed.at[index], self.base + index, {Z_AXIS: self.other})
        add_strips(dst, (*self.ring.terms(self.z, index), self.pair_landed.at[index]))

    def drain(self, index):
        self.ring.drain(index)
        self.copies.sent(self.pair_sums.at[index], self.base + index, {Z_AXIS: self.other})


class RowGather:
    def __init__(self, copies, count, buffer):
        self.copies, self.count, self.buffer = copies, count, buffer
        self.base = copies.slots(7 * count)
        self.here, self.plus, self.minus, self.opposite = around(X_AXIS)
        self.z = lax.axis_index(Z_AXIS)
        self.other = 1 - self.z

    def send(self, place, z, kind, index, peer):
        ref = self.buffer.at[place, z, index]
        self.copies.send(ref, ref, self.base + kind * self.count + index, peer)

    def wait(self, place, z, kind, index):
        ref = self.buffer.at[place, z, index]
        slot = self.base + kind * self.count + index
        self.copies.arrived(ref, slot, {Z_AXIS: self.other})

    def start(self, index):
        self.send(self.here, self.z, 0, index, {Z_AXIS: self.other})
        self.send(self.here, self.z, 1, index, {X_AXIS: self.plus})
        self.send(self.here, self.z, 2, index, {X_AXIS: self.minus})

    def pair(self, index):
        self.wait(self.here, self.other, 0, index)
        self.send(self.here, self.other, 3, index, {X_AXIS: self.plus})
        self.send(self.here, self.other, 4, index, {X_AXIS: self.minus})

    def forward(self, index):
        self.wait(self.minus, self.z, 1, index)
        self.wait(self.minus, self.other, 3, index)
        self.send(self.minus, 0, 5, index, {X_AXIS: self.plus})
        self.wait(self.plus, self.z, 2, index)
        self.wait(self.plus, self.other, 4, index)
        self.send(self.plus, 1, 6, index, {X_AXIS: self.minus})

    def finish(self, index):
        self.wait(self.opposite, 0, 5, index)
        self.wait(self.opposite, 1, 6, index)

    def drain(self, index):
        for kind in range(7):
            ref = self.buffer.at[0, 0, index]
            slot = self.base + kind * self.count + index
            self.copies.sent(ref, slot, {Z_AXIS: self.other})


class RingGather:
    def __init__(self, copies, axis, whole, half):
        self.copies, self.axis, self.whole, self.half = copies, axis, whole, half
        self.base = copies.slots(4)
        self.here, self.plus, self.minus, self.opposite = around(axis)

    def send(self, ref, kind, peer):
        self.copies.send(ref, ref, self.base + kind, {self.axis: peer})

    def wait(self, ref, kind):
        self.copies.arrived(ref, self.base + kind, {self.axis: self.plus})

    def start(self):
        self.send(self.whole(self.here), 0, self.plus)
        self.send(self.whole(self.here), 1, self.minus)

    def from_minus(self):
        self.wait(self.whole(self.minus), 0)
        self.send(self.half(self.minus, 0), 2, self.plus)

    def from_plus(self):
        self.wait(self.whole(self.plus), 1)
        self.send(self.half(self.plus, 1), 3, self.minus)

    def finish(self):
        self.wait(self.half(self.opposite, 0), 2)
        self.wait(self.half(self.opposite, 1), 3)

    def drain(self):
        for kind in range(4):
            ref = self.whole(0) if kind < 2 else self.half(0, 0)
            self.copies.sent(ref, self.base + kind, {self.axis: self.plus})


class ColGather:
    def __init__(self, copies, buffer):
        here, plus, minus, opposite = around(H_AXIS)
        y = lax.axis_index(Y_AXIS)
        self.outer = RingGather(
            copies,
            H_AXIS,
            lambda place: buffer.at[place, y],
            lambda place, half: buffer.at[place, y, half],
        )
        self.inner = [
            RingGather(
                copies,
                Y_AXIS,
                lambda place, layer=layer: buffer.at[layer, place],
                lambda place, half, layer=layer: buffer.at[layer, place, half],
            )
            for layer in (here, minus, plus, opposite)
        ]

    def start(self):
        self.outer.start()
        self.inner[0].start()

    def run(self):
        self.outer.from_minus()
        self.inner[1].start()
        self.outer.from_plus()
        self.inner[2].start()
        self.inner[0].from_minus()
        self.inner[0].from_plus()
        self.outer.finish()
        self.inner[3].start()
        for inner in self.inner[1:]:
            inner.from_minus()
            inner.from_plus()
        for inner in self.inner:
            inner.finish()

    def drain(self):
        self.outer.drain()
        for inner in self.inner:
            inner.drain()


def step_kernel(
    tokens,
    target,
    gate_weight,
    up_weight,
    down_weight,
    probe_gate,
    probe_up,
    probe_down,
    grad_gate_out,
    grad_up_out,
    grad_down_out,
    curv_gate_out,
    curv_up_out,
    curv_down_out,
    sums_out,
    wide,
    tall,
    proj,
    down,
    x,
    tgt,
    part,
    part_landed,
    pair_sums,
    pair_landed,
    pre,
    hid,
    outs,
    outs_landed,
    layer_sums,
    layer_landed,
    final,
    err,
    back,
    back_landed,
    back_pair,
    back_pair_landed,
    d_hid,
    d_pre,
    grads,
    grads_landed,
    grads_down,
    grads_down_landed,
    tiles,
    tiles_landed,
    send_sems,
    recv_sems,
):
    copies = Copies(send_sems, recv_sems)
    core = lax.axis_index(CORE_AXIS)
    other_core = 1 - core
    x_here, x_plus, x_minus, x_opposite = around(X_AXIS)
    y_here, y_plus, y_minus, y_opposite = around(Y_AXIS)
    h_here, h_plus, h_minus, h_opposite = around(H_AXIS)
    z_here = lax.axis_index(Z_AXIS)
    partner = {CORE_AXIS: other_core}

    barrier = pltpu.get_barrier_semaphore()
    peers = [partner, {Z_AXIS: 1 - z_here}]
    for axis in (X_AXIS, Y_AXIS, H_AXIS):
        peers += [{axis: place} for place in around(axis)[1:]]
    for peer in peers:
        pl.semaphore_signal(barrier, inc=1, device_id=peer, device_id_type=MESH)

    own_rows = pl.ds(pl.multiple_of(core * HALF, HALF), HALF)
    other_rows = pl.ds(pl.multiple_of(other_core * HALF, HALF), HALF)
    x[h_here, y_here, core] = tokens[own_rows, :]
    tgt[core] = target[own_rows, :]

    def lay_out(source, index):
        wide[:, FEATS:] = jnp.zeros((FEATS, 3 * LANES - FEATS), BF16)
        wide[:, :UNITS] = source
        proj[core, index] = wide[...].T[:PADDED]

    def sign(ref):
        return (2 * ref[...] - 1).astype(F32).astype(BF16)

    lay_out(gate_weight[...], 0)
    lay_out(up_weight[...], 1)
    lay_out(sign(probe_gate), 2)
    lay_out(sign(probe_up), 3)
    rest = jnp.zeros((32, FEATS), BF16)
    down[core, 0, PADDED - 32 :] = rest
    down[core, 1, PADDED - 32 :] = rest
    down[core, 0, :UNITS] = down_weight[...]
    down[core, 1, :UNITS] = sign(probe_down)

    pl.semaphore_wait(barrier, len(peers))
    near = copies.slots(6)
    copies.send(tokens.at[other_rows], x.at[h_here, y_here, core], near, partner)
    copies.send(proj.at[core], proj.at[core], near + 1, partner)
    copies.send(target.at[other_rows], tgt.at[core], near + 2, partner)
    copies.send(down.at[core], down.at[core], near + 3, partner)

    copies.arrived(x.at[h_here, y_here, other_core], near, partner)
    x_gather = ColGather(copies, x)
    x_gather.start()
    x_gather.run()
    copies.arrived(proj.at[other_core], near + 1, partner)

    def token_block(ref, place, *rest):
        return [
            ref[(place, slice(None), *rest, half)].reshape(RING * HALF, FEATS) for half in range(2)
        ]

    row_sum = RowSum(copies, 4, part, part_landed, pair_sums, pair_landed)

    def project(index, place):
        left, right = token_block(x, place)
        both = dot_nt(proj[0, index], left) + dot_nt(proj[1, index], right)
        both = both.astype(BF16)
        part[place, 0, index] = both[:, :LANES]
        part[place, 1, index] = both[:, LANES:]

    def project_all(index, carry):
        project(index, x_opposite)
        row_sum.ring.send_opposite(index)
        project(index, x_plus)
        row_sum.ring.send_plus(index)
        project(index, x_minus)
        row_sum.ring.send_minus(index)
        project(index, x_here)
        return carry

    def each(count, step):
        def body(index, carry):
            step(index)
            return carry

        lax.fori_loop(0, count, body, 0)

    lax.fori_loop(0, 4, project_all, 0)
    each(4, row_sum.ring.forward)
    each(4, row_sum.pair)
    each(4, lambda index: row_sum.finish(pre.at[index], index))

    def strips(step):
        def body(index, carry):
            step(pl.ds(pl.multiple_of(index * STRIP, STRIP), STRIP))
            return carry

        lax.fori_loop(0, PADDED // STRIP, body, 0)

    def hide(rows):
        pre_gate, pre_up = pre[0, rows, :], pre[1, rows, :]
        dot_gate, dot_up = pre[2, rows, :], pre[3, rows, :]
        sig = jax.nn.sigmoid(pre_gate)
        act = pre_gate * sig
        slope = sig * (1.0 + pre_gate * (1.0 - sig))
        hid[x_here, z_here, 0, rows, :] = (act * pre_up).astype(BF16)
        hid[x_here, z_here, 1, rows, :] = (slope * dot_gate * pre_up + act * dot_up).astype(BF16)

    strips(hide)
    hid_gather = RowGather(copies, 2, hid)
    each(2, hid_gather.start)
    each(2, hid_gather.pair)
    copies.arrived(down.at[other_core], near + 3, partner)

    out_sum = RingSum(
        copies,
        Y_AXIS,
        4,
        lambda place, half, layer: outs.at[layer[1], place, half],
        lambda kind, layer: outs_landed.at[kind, layer[0]],
        add_blocks,
    )
    out_sum.slot = lambda kind, layer: out_sum.base + kind * 4 + layer[0]

    def whole_units(ref, place, index):
        return jnp.concatenate([ref[place, 0, index], ref[place, 1, index]], axis=1)

    def expand(place):
        plain = whole_units(hid, place, 0)
        tangent = whole_units(hid, place, 1)
        for half in range(2):
            value = dot_tn(plain, down[half, 0])
            along = dot_tn(tangent, down[half, 0]) + dot_tn(plain, down[half, 1])
            value = value.astype(BF16).reshape(RING, HALF, FEATS)
            along = along.astype(BF16).reshape(RING, HALF, FEATS)
            for block in range(RING):
                outs[place, block, 0, half] = value[block]
                outs[place, block, 1, half] = along[block]

    layers = [(0, x_here), (1, x_minus), (2, x_plus), (3, x_opposite)]

    def expand_and_send(layer):
        expand(layer[1])
        out_sum.send_opposite(layer)
        out_sum.send_plus(layer)
        out_sum.send_minus(layer)

    expand_and_send(layers[0])
    each(2, hid_gather.forward)
    expand_and_send(layers[1])
    expand_and_send(layers[2])
    out_sum.forward(layers[0])
    each(2, hid_gather.finish)
    expand_and_send(layers[3])
    for layer in layers[1:]:
        out_sum.forward(layer)
    for layer in layers:
        out_sum.wait_terms(layer)
        for half in range(2):
            add_blocks(layer_sums.at[layer[1], half], out_sum.terms(half, layer))

    layer_sum = RingSum(
        copies,
        H_AXIS,
        1,
        lambda place, half, index: layer_sums.at[place, half],
        lambda kind, index: layer_landed.at[kind],
        add_blocks,
    )
    layer_sum.send_opposite(0)
    layer_sum.send_plus(0)
    layer_sum.send_minus(0)
    layer_sum.forward(0)
    layer_sum.wait_terms(0)
    copies.arrived(tgt.at[other_core], near + 2, partner)
    for half in range(2):
        add_blocks(final.at[half], layer_sum.terms(half, 0))
    for side in range(2):
        value = final[0, side] - tgt[side].astype(F32)
        err[h_here, y_here, 0, side] = value.astype(BF16)
        err[h_here, y_here, 1, side] = final[1, side].astype(BF16)

    err_gather = ColGather(copies, err)
    err_gather.start()
    err_gather.run()

    back_sum = RowSum(copies, 2, back, back_landed, back_pair, back_pair_landed)

    def turn_back(place):
        plain = token_block(err, place, 0)
        tangent = token_block(err, place, 1)
        value = dot_nt(down[0, 0], plain[0]) + dot_nt(down[1, 0], plain[1])
        along = dot_nt(down[0, 0], tangent[0]) + dot_nt(down[1, 0], tangent[1])
        along = along + dot_nt(down[0, 1], plain[0]) + dot_nt(down[1, 1], plain[1])
        for index, whole in enumerate((value, along)):
            whole = whole.astype(BF16)
            back[place, 0, index] = whole[:, :LANES]
            back[place, 1, index] = whole[:, LANES:]

    turn_back(x_opposite)
    each(2, back_sum.ring.send_opposite)
    turn_back(x_plus)
    each(2, back_sum.ring.send_plus)
    turn_back(x_minus)
    each(2, back_sum.ring.send_minus)
    turn_back(x_here)
    each(2, back_sum.ring.forward)
    each(2, back_sum.pair)
    each(2, lambda index: back_sum.finish(d_hid.at[index], index))

    def slopes(rows):
        pre_gate, pre_up = pre[0, rows, :], pre[1, rows, :]
        dot_gate, dot_up = pre[2, rows, :], pre[3, rows, :]
        d_hidden, d_hidden_dot = d_hid[0, rows, :], d_hid[1, rows, :]
        sig = jax.nn.sigmoid(pre_gate)
        act = pre_gate * sig
        slope = sig * (1.0 + pre_gate * (1.0 - sig))
        bend = sig * (1.0 - sig) * (2.0 + pre_gate * (1.0 - 2.0 * sig))
        dd_gate = (
            d_hidden_dot * pre_up * slope
            + d_hidden * dot_up * slope
            + d_hidden * pre_up * bend * dot_gate
        )
        dd_up = d_hidden_dot * act + d_hidden * slope * dot_gate
        d_pre[x_here, z_here, 0, rows, :] = (d_hidden * pre_up * slope).astype(BF16)
        d_pre[x_here, z_here, 1, rows, :] = (d_hidden * act).astype(BF16)
        d_pre[x_here, z_here, 2, rows, :] = dd_gate.astype(BF16)
        d_pre[x_here, z_here, 3, rows, :] = dd_up.astype(BF16)

    strips(slopes)
    pre_gather = RowGather(copies, 4, d_pre)
    each(4, pre_gather.start)
    each(4, pre_gather.pair)
    each(4, pre_gather.forward)

    def down_grads(side):
        plain_sum = jnp.zeros((PADDED, FEATS), F32)
        along_sum = jnp.zeros((PADDED, FEATS), F32)
        for place in range(RING):
            plain = whole_units(hid, place, 0)
            tangent = whole_units(hid, place, 1)
            err_block = err[place, :, 0, side].reshape(RING * HALF, FEATS)
            dot_block = err[place, :, 1, side].reshape(RING * HALF, FEATS)
            plain_sum = plain_sum + dot_nn(plain, err_block)
            along_sum = along_sum + dot_nn(tangent, err_block) + dot_nn(plain, dot_block)
        grads_down[side, 0] = plain_sum
        grads_down[side, 1] = along_sum

    down_grads(other_core)
    copies.send(grads_down.at[other_core], grads_down_landed, near + 4, partner)
    down_grads(core)

    each(4, pre_gather.finish)

    def pre_grads(side):
        def one(index):
            total = jnp.zeros((PADDED, FEATS), F32)
            for place in range(RING):
                tokens_block = x[place, :, side].reshape(RING * HALF, FEATS)
                total = total + dot_nn(whole_units(d_pre, place, index), tokens_block)
            grads[side, index] = total

        each(4, one)

    pre_grads(other_core)
    copies.send(grads.at[other_core], grads_landed, near + 5, partner)
    pre_grads(core)

    def squares(values):
        return jnp.sum(values * values, axis=0, keepdims=True)

    copies.arrived(grads_down_landed, near + 4, partner)
    grad = grads_down[core, 0] + grads_down_landed[0]
    hess = grads_down[core, 1] + grads_down_landed[1]
    grad_down_out[...] = grad[:UNITS]
    grad_sum = squares(grad)
    curv = curvature(down[core, 1].astype(F32), hess)
    curv_down_out[...] = curv[:UNITS]
    curv_sum = squares(curv)

    tall[PADDED - 32 :] = jnp.zeros((3 * LANES - PADDED + 32, FEATS), F32)

    def turned(values, out):
        tall[:PADDED] = values
        out[...] = tall[...].T[:, :UNITS]

    copies.arrived(grads_landed, near + 5, partner)
    for index, (grad_out, curv_out) in enumerate(
        ((grad_gate_out, curv_gate_out), (grad_up_out, curv_up_out))
    ):
        grad = grads[core, index] + grads_landed[index]
        turned(grad, grad_out)
        grad_sum = grad_sum + squares(grad)
        hess = grads[core, 2 + index] + grads_landed[2 + index]
        curv = curvature(proj[core, 2 + index].astype(F32), hess)
        turned(curv, curv_out)
        curv_sum = curv_sum + squares(curv)

    lane = lax.broadcasted_iota(jnp.int32, (8, LANES), 1)
    grad_sum = jnp.sum(grad_sum, axis=1, keepdims=True)
    curv_sum = jnp.sum(curv_sum, axis=1, keepdims=True)
    tiles[0] = jnp.where(lane == 0, grad_sum, jnp.where(lane == 1, curv_sum, 0.0))

    stages = [
        [partner],
        [{Z_AXIS: 1 - z_here}],
        [{X_AXIS: x_plus}, {X_AXIS: x_opposite}, {X_AXIS: x_minus}],
        [{Y_AXIS: y_plus}, {Y_AXIS: y_opposite}, {Y_AXIS: y_minus}],
        [{H_AXIS: h_plus}, {H_AXIS: h_opposite}, {H_AXIS: h_minus}],
    ]
    small = copies.slots(3 * len(stages))
    for stage, receivers in enumerate(stages):
        for index, peer in enumerate(receivers):
            slot = small + 3 * stage + index
            copies.send(tiles.at[stage], tiles_landed.at[stage, index], slot, peer)
        total = tiles[stage]
        for index, peer in enumerate(receivers):
            copies.arrived(tiles_landed.at[stage, index], small + 3 * stage + index, peer)
            total = total + tiles_landed[stage, index]
        tiles[stage + 1] = total
    sums_out[...] = tiles[len(stages)]

    copies.sent(x.at[0, 0, 0], near, partner)
    copies.sent(proj.at[0], near + 1, partner)
    copies.sent(tgt.at[0], near + 2, partner)
    copies.sent(down.at[0], near + 3, partner)
    copies.sent(grads_down_landed, near + 4, partner)
    copies.sent(grads_landed, near + 5, partner)
    x_gather.drain()
    err_gather.drain()
    each(4, row_sum.drain)
    each(2, back_sum.drain)
    each(2, hid_gather.drain)
    each(4, pre_gather.drain)
    for layer in layers:
        out_sum.drain(layer)
    layer_sum.drain(0)
    for stage, receivers in enumerate(stages):
        for index, peer in enumerate(receivers):
            copies.sent(tiles.at[stage], small + 3 * stage + index, peer)


SLOTS = 240


def whole_step(*operands):
    natural = jax.ShapeDtypeStruct((FEATS, UNITS), F32)
    turned = jax.ShapeDtypeStruct((UNITS, FEATS), F32)
    units = (PADDED, LANES)
    block = (2, HALF, FEATS)
    return pl.pallas_call(
        step_kernel,
        out_shape=(
            natural,
            natural,
            turned,
            natural,
            natural,
            turned,
            jax.ShapeDtypeStruct((8, LANES), F32),
        ),
        in_specs=[pl.BlockSpec(memory_space=pltpu.VMEM)] * 8,
        out_specs=[pl.BlockSpec(memory_space=pltpu.VMEM)] * 7,
        scratch_shapes=[
            pltpu.VMEM((FEATS, 3 * LANES), BF16),
            pltpu.VMEM((3 * LANES, FEATS), F32),
            pltpu.VMEM((2, 4, PADDED, FEATS), BF16),
            pltpu.VMEM((2, 2, PADDED, FEATS), BF16),
            pltpu.VMEM((RING, RING, *block), BF16),
            pltpu.VMEM(block, BF16),
            pltpu.VMEM((RING, 2, 4, *units), BF16),
            pltpu.VMEM((6, 4, *units), BF16),
            pltpu.VMEM((4, *units), BF16),
            pltpu.VMEM((4, *units), BF16),
            pltpu.VMEM((4, *units), F32),
            pltpu.VMEM((RING, 2, 2, *units), BF16),
            pltpu.VMEM((RING, RING, 2, *block), BF16),
            pltpu.VMEM((6, RING, *block), BF16),
            pltpu.VMEM((RING, 2, *block), BF16),
            pltpu.VMEM((6, *block), BF16),
            pltpu.VMEM((2, *block), F32),
            pltpu.VMEM((RING, RING, 2, *block), BF16),
            pltpu.VMEM((RING, 2, 2, *units), BF16),
            pltpu.VMEM((6, 2, *units), BF16),
            pltpu.VMEM((2, *units), BF16),
            pltpu.VMEM((2, *units), BF16),
            pltpu.VMEM((2, *units), F32),
            pltpu.VMEM((RING, 2, 4, *units), BF16),
            pltpu.VMEM((2, 4, PADDED, FEATS), F32),
            pltpu.VMEM((4, PADDED, FEATS), F32),
            pltpu.VMEM((2, 2, PADDED, FEATS), F32),
            pltpu.VMEM((2, PADDED, FEATS), F32),
            pltpu.VMEM((6, 8, LANES), F32),
            pltpu.VMEM((5, 3, 8, LANES), F32),
            pltpu.SemaphoreType.DMA((SLOTS,)),
            pltpu.SemaphoreType.DMA((SLOTS,)),
        ],
        compiler_params=pltpu.CompilerParams(
            collective_id=0, has_side_effects=True, vmem_limit_bytes=60 * 1024 * 1024
        ),
    )(*operands)


def body(
    tokens,
    target,
    gate_weight,
    up_weight,
    down_weight,
    probe_gate,
    probe_up,
    probe_down,
    first_gate,
    first_up,
    first_down,
    second_gate,
    second_up,
    second_down,
):
    grad_gate, grad_up, grad_down, curv_gate, curv_up, curv_down, sums = whole_step(
        tokens, target, gate_weight, up_weight, down_weight, probe_gate, probe_up, probe_down
    )
    count = 3.0 * D * FF
    rms_grad = jnp.sqrt(sums[0, 0] / count + 1e-06)
    rms_curv = jnp.sqrt(sums[0, 1] / count + 1e-06)
    fix_first = 1.0 - 0.9**STEP
    fix_second = 1.0 - 0.95**STEP
    firsts = []
    seconds = []
    updates = []
    for grad, curv, first, second in (
        (grad_gate, curv_gate, first_gate, second_gate),
        (grad_up, curv_up, first_up, second_up),
        (grad_down, curv_down, first_down, second_down),
    ):
        new_first = 0.9 * first + 0.1 * (grad / rms_grad)
        scaled = curv / rms_curv
        new_second = 0.95 * second + 0.05 * (scaled * scaled)
        firsts.append(new_first)
        seconds.append(new_second)
        updates.append(new_first / fix_first / (jnp.sqrt(new_second / fix_second) + 1e-08))
    return (*firsts, *seconds, *updates)


def solution(mesh):
    torus = Mesh(mesh.devices.reshape(4, 2, 2, 4, 4), (*ROW, *COL))
    feats, units = P(ROW, COL), P(COL, ROW)
    in_specs = (units, units, feats, feats, units) + (feats, feats, units) * 3
    out_specs = (feats, feats, units) * 3
    return jax.shard_map(body, mesh=torus, in_specs=in_specs, out_specs=out_specs, check_vma=False)
```

time: 560 us -> 194 us (0.35)
  blocking collectives: 182 us -> 0 us
  waiting for transfers between devices: 178 us -> 0 us
  Pallas kernels: 0 us -> 173 us
  local copies, waits for them, and re-layouts: 109 us -> 15.4 us
  other arithmetic: 34.8 us -> 3.14 us
  matrix products: 21.1 us -> 0 us
  between operations: 19.6 us -> 2.1 us
  starting transfers between devices: 11.6 us -> 0 us
    pallas_call x0 -> x1, Pallas kernels: none -> 173 us  [whole_step(): pl.pallas_call(step_kernel, out_shape=(natural, natural, turned, natural,...]
    all_to_all x3 -> x0, blocking collectives: 140 us -> none  [the longest x2 101 us: sent_and_summed(): parts = lax.all_to_all(split_up(shard, dim, length), axis, 0, 0, tiled=True)]
    all_gather x3 -> x0, waiting for transfers between devices: 115 us -> none  [the longest x1 54.1 us: body(): err_all = lax.all_gather(errors, COL, axis=0, tiled=True)]
    all_to_all x2 -> x0, waiting for transfers between devices: 63.7 us -> none  [sent_and_summed(): parts = lax.all_to_all(split_up(shard, dim, length), axis, 0, 0, tiled=True)]
    reshape x3 -> x0, local copies, waits for them, and re-layouts: 56.5 us -> none  [block_mean(): means = values.reshape(height // 4, 4, breadth // 4, 4).mean(axis=(1, 3))]
    psum x5 -> x0, blocking collectives: 41.8 us -> none  [over_axes(): return functools.reduce(lax.psum, axes, shard)]
    mul x6 -> x0, local copies, waits for them, and re-layouts: 31.8 us -> none  [the longest x3 31.6 us: body(): new_second = 0.95 * second + 0.05 * (scaled * scaled)]
    reduce_sum x10 -> x0, other arithmetic: 22.6 us -> none  [the longest x3 15.2 us: block_mean(): means = values.reshape(height // 4, 4, breadth // 4, 4).mean(axis=(1, 3))]
  transfers between devices with their start and end apart: 5 -> 0, of which waited for: 5 -> 0; matrix products, arithmetic and copies ran while one was open for 6% -> 0% of each run, Pallas kernels for 0% -> 0%
where the time goes in v2:
time: 194 us
  Pallas kernels  173 us (89%)
  local copies, waits for them, and re-layouts  15.4 us (8%)
  other arithmetic  3.14 us (2%)
  between operations  2.1 us (1%)
    pallas_call x1, Pallas kernels, whole_step(): pl.pallas_call(step_kernel, out_shape=(natural, natural, turned, natural,...  173 us
    unnamed x36, local copies, waits for them, and re-layouts  14.1 us

profile of v2, /device:TPU:32, one launch (start us, length us, event | category | flops | bytes accessed | tf_op | source)
XLA Modules:
  0.0 193.7 jit_solution(11845064175464210109)
XLA Ops:
  0.6 0.0 copy-start.4
  0.7 1.9 %copy.26.probe_gate = s32[256,344]{1,0:T(8,128)} copy(s32[256,344]{0,1:T(8,128)} %param.19) | data formatting | bytes 704512 | tf_op args[5]
  2.6 0.0 copy-done.4
  2.6 0.0 copy-start.9
  2.6 0.9 copy.27.probe_up
  3.5 0.0 copy-done.9
  3.5 0.8 copy.24.gate_weight
  4.3 0.1 copy-done.10
  4.4 0.8 copy.25.up_weight
  5.3 173.1 %shard_map.205 = (f32[256,344]{1,0:T(8,128)}, f32[256,344]{1,0:T(8,128)}, f32[344,256]{1,0:T(8,128)}, f32[256,344]{1,0:T(8,128)}, f32[256,344]{1,0:T(8,128)}, /*index=5*/f32[344,256]{1,0:T(8,128)}, f32[8,128]{1,0:T(8,128)}) custom-call(bf16[128,256]{1,0:T(8,128)(2,1)} %tokens.1, bf16[128,256]{1,0:T(8,128)(2,1)} %target.1, ...), custom_call_target="tpu_custom_call" | custom-call | tf_op jit(solution)/shard_map/pallas_call | solution.py:729
  178.3 1.3 fusion
  181.1 0.0 copy-done.5
  181.1 0.0 copy-start.6
  181.1 0.2 copy.23
  181.3 0.8 copy-done.6
  182.1 0.2 copy.28
  182.2 0.8 copy-done.7
  183.0 0.2 copy.29
  183.2 0.8 copy-done.8
  184.0 0.9 copy.30
  184.9 2.0 %add_divide_fusion = (f32[256,344]{1,0:T(8,128)S(1)}, f32[256,344]{1,0:T(8,128)S(1)}, f32[256,344]{1,0:T(8,128)S(1)}, f32[256,344]{1,0:T(8,128)S(1)}, f32[256,344]{1,0:T(8,128)S(1)}, /*index=5*/f32[256,344]{1,0:T(8,128)S(1)}) fusion(f32[256,344]{1,0:T(8,128)} %get-tuple-element.21, f32[]{:T(128)} %bitcast.1, f32[256,344]{1,0:T(8,128)} %copy.30, ...), kind=kLoop, calls=%fused_computation | loop fusion | flops 2289664 | bytes 4931592 | tf_op jit(solution)/shard_map/div | solution.py:819
  187.0 0.9 copy.31
  187.9 0.9 copy.32
  188.7 0.9 copy.33
  189.6 0.9 copy.34
  190.5 0.9 copy.35
  191.4 0.9 copy.36
  192.3 0.0 copy-done.2
  192.3 0.0 copy-done.3
  192.3 0.1 copy-done
  192.4 0.2 copy-done.1
  192.6 1.1 add_divide_fusion.2
  (8 shorter events, 0.0 us)
Async XLA Ops:
  0.6 2.0 %copy-start.4 = (s32[256,344]{0,1:T(8,128)S(1)}, s32[256,344]{0,1:T(8,128)}, u32[]{:S(2)}) copy-start(s32[256,344]{0,1:T(8,128)} %param.20) | copy-start | bytes 1056772
  2.6 0.9 copy-start.9
  3.5 0.9 copy-start.10
  5.3 175.8 %copy-start.5 = (f32[256,344]{0,1:T(8,128)S(1)}, f32[256,344]{0,1:T(8,128)}, u32[]{:S(2)}) copy-start(f32[256,344]{0,1:T(8,128)} %param.22) | copy-start | bytes 1056772
  181.1 1.0 copy-start.6
  182.1 1.0 copy-start.7
  183.0 1.0 copy-start.8
  190.5 1.8 copy-start.2
  190.5 1.8 copy-start.3
  191.4 1.0 copy-start
  191.4 1.2 copy-start.1

commit v3 on v2

--- a/solution.py
+++ b/solution.py
@@ -133,6 +133,22 @@
         ref = self.landed(kind, index)
         self.copies.arrived(ref, self.slot(kind, index), {self.axis: self.plus})
 
+    def send_for(self, place, index):
+        role = lax.rem(place - self.here + RING, RING)
+
+        @pl.when(role == 1)
+        def _():
+            self.send(self.block(place, 1, index), 3, index, self.plus)
+
+        @pl.when(role == 2)
+        def _():
+            self.send(self.block(place, 0, index), 0, index, self.plus)
+            self.send(self.block(place, 1, index), 1, index, self.minus)
+
+        @pl.when(role == 3)
+        def _():
+            self.send(self.block(place, 0, index), 4, index, self.minus)
+
     def send_opposite(self, index):
         self.send(self.block(self.opposite, 0, index), 0, index, self.plus)
         self.send(self.block(self.opposite, 1, index), 1, index, self.minus)
@@ -275,6 +291,10 @@
     def from_plus(self):
         self.wait(self.whole(self.plus), 1)
         self.send(self.half(self.plus, 1), 3, self.minus)
+
+    def forward(self):
+        self.from_minus()
+        self.from_plus()
 
     def finish(self):
         self.wait(self.half(self.opposite, 0), 2)
@@ -305,25 +325,32 @@
             )
             for layer in (here, minus, plus, opposite)
         ]
+        self.places = (here, minus, plus, opposite)
 
     def start(self):
         self.outer.start()
         self.inner[0].start()
 
-    def run(self):
+    def run(self, use):
+        here, minus, plus, opposite = self.inner
+        here.forward()
         self.outer.from_minus()
-        self.inner[1].start()
+        minus.start()
         self.outer.from_plus()
-        self.inner[2].start()
-        self.inner[0].from_minus()
-        self.inner[0].from_plus()
+        plus.start()
+        here.finish()
+        use(self.places[0])
+        minus.forward()
+        plus.forward()
         self.outer.finish()
-        self.inner[3].start()
-        for inner in self.inner[1:]:
-            inner.from_minus()
-            inner.from_plus()
-        for inner in self.inner:
-            inner.finish()
+        opposite.start()
+        minus.finish()
+        use(self.places[1])
+        plus.finish()
+        use(self.places[2])
+        opposite.forward()
+        opposite.finish()
+        use(self.places[3])
 
     def drain(self):
         self.outer.drain()
@@ -347,8 +374,6 @@
     curv_up_out,
     curv_down_out,
     sums_out,
-    wide,
-    tall,
     proj,
     down,
     x,
@@ -401,26 +426,22 @@
     x[h_here, y_here, core] = tokens[own_rows, :]
     tgt[core] = target[own_rows, :]
 
-    def lay_out(source, index):
-        wide[:, FEATS:] = jnp.zeros((FEATS, 3 * LANES - FEATS), BF16)
-        wide[:, :UNITS] = source
-        proj[core, index] = wide[...].T[:PADDED]
-
     def sign(ref):
         return (2 * ref[...] - 1).astype(F32).astype(BF16)
 
-    lay_out(gate_weight[...], 0)
-    lay_out(up_weight[...], 1)
-    lay_out(sign(probe_gate), 2)
-    lay_out(sign(probe_up), 3)
-    rest = jnp.zeros((32, FEATS), BF16)
-    down[core, 0, PADDED - 32 :] = rest
-    down[core, 1, PADDED - 32 :] = rest
-    down[core, 0, :UNITS] = down_weight[...]
-    down[core, 1, :UNITS] = sign(probe_down)
+    def lay_out(dst, index, values):
+        dst[core, index, PADDED - 32 :] = jnp.zeros((32, FEATS), BF16)
+        dst[core, index, :UNITS] = values
+
+    lay_out(proj, 0, gate_weight[...])
+    lay_out(proj, 1, up_weight[...])
+    lay_out(proj, 2, sign(probe_gate))
+    lay_out(proj, 3, sign(probe_up))
+    lay_out(down, 0, down_weight[...])
+    lay_out(down, 1, sign(probe_down))
 
     pl.semaphore_wait(barrier, len(peers))
-    near = copies.slots(6)
+    near = copies.slots(9)
     copies.send(tokens.at[other_rows], x.at[h_here, y_here, core], near, partner)
     copies.send(proj.at[core], proj.at[core], near + 1, partner)
     copies.send(target.at[other_rows], tgt.at[core], near + 2, partner)
@@ -429,7 +450,6 @@
     copies.arrived(x.at[h_here, y_here, other_core], near, partner)
     x_gather = ColGather(copies, x)
     x_gather.start()
-    x_gather.run()
     copies.arrived(proj.at[other_core], near + 1, partner)
 
     def token_block(ref, place, *rest):
@@ -446,16 +466,6 @@
         part[place, 0, index] = both[:, :LANES]
         part[place, 1, index] = both[:, LANES:]
 
-    def project_all(index, carry):
-        project(index, x_opposite)
-        row_sum.ring.send_opposite(index)
-        project(index, x_plus)
-        row_sum.ring.send_plus(index)
-        project(index, x_minus)
-        row_sum.ring.send_minus(index)
-        project(index, x_here)
-        return carry
-
     def each(count, step):
         def body(index, carry):
             step(index)
@@ -463,10 +473,16 @@
 
         lax.fori_loop(0, count, body, 0)
 
-    lax.fori_loop(0, 4, project_all, 0)
+    def project_and_send(place):
+        def one(index):
+            project(index, place)
+            row_sum.ring.send_for(place, index)
+
+        each(4, one)
+
+    x_gather.run(project_and_send)
     each(4, row_sum.ring.forward)
     each(4, row_sum.pair)
-    each(4, lambda index: row_sum.finish(pre.at[index], index))
 
     def strips(step):
         def body(index, carry):
@@ -476,17 +492,25 @@
         lax.fori_loop(0, PADDED // STRIP, body, 0)
 
     def hide(rows):
+        pre_gate, pre_up = pre[0, rows, :], pre[1, rows, :]
+        act = pre_gate * jax.nn.sigmoid(pre_gate)
+        hid[x_here, z_here, 0, rows, :] = (act * pre_up).astype(BF16)
+
+    def hide_dot(rows):
         pre_gate, pre_up = pre[0, rows, :], pre[1, rows, :]
         dot_gate, dot_up = pre[2, rows, :], pre[3, rows, :]
         sig = jax.nn.sigmoid(pre_gate)
         act = pre_gate * sig
         slope = sig * (1.0 + pre_gate * (1.0 - sig))
-        hid[x_here, z_here, 0, rows, :] = (act * pre_up).astype(BF16)
         hid[x_here, z_here, 1, rows, :] = (slope * dot_gate * pre_up + act * dot_up).astype(BF16)
 
+    hid_gather = RowGather(copies, 2, hid)
+    each(2, lambda index: row_sum.finish(pre.at[index], index))
     strips(hide)
-    hid_gather = RowGather(copies, 2, hid)
-    each(2, hid_gather.start)
+    hid_gather.start(0)
+    each(2, lambda index: row_sum.finish(pre.at[2 + index], 2 + index))
+    strips(hide_dot)
+    hid_gather.start(1)
     each(2, hid_gather.pair)
     copies.arrived(down.at[other_core], near + 3, partner)
 
@@ -523,20 +547,6 @@
         out_sum.send_plus(layer)
         out_sum.send_minus(layer)
 
-    expand_and_send(layers[0])
-    each(2, hid_gather.forward)
-    expand_and_send(layers[1])
-    expand_and_send(layers[2])
-    out_sum.forward(layers[0])
-    each(2, hid_gather.finish)
-    expand_and_send(layers[3])
-    for layer in layers[1:]:
-        out_sum.forward(layer)
-    for layer in layers:
-        out_sum.wait_terms(layer)
-        for half in range(2):
-            add_blocks(layer_sums.at[layer[1], half], out_sum.terms(half, layer))
-
     layer_sum = RingSum(
         copies,
         H_AXIS,
@@ -545,9 +555,27 @@
         lambda kind, index: layer_landed.at[kind],
         add_blocks,
     )
-    layer_sum.send_opposite(0)
-    layer_sum.send_plus(0)
-    layer_sum.send_minus(0)
+
+    def complete(layer):
+        out_sum.wait_terms(layer)
+        for half in range(2):
+            add_blocks(layer_sums.at[layer[1], half], out_sum.terms(half, layer))
+        layer_sum.send_for(layer[1], 0)
+
+    expand_and_send(layers[0])
+    each(2, hid_gather.forward)
+    out_sum.forward(layers[0])
+    expand_and_send(layers[1])
+    expand_and_send(layers[2])
+    complete(layers[0])
+    out_sum.forward(layers[1])
+    out_sum.forward(layers[2])
+    each(2, hid_gather.finish)
+    expand_and_send(layers[3])
+    complete(layers[1])
+    complete(layers[2])
+    out_sum.forward(layers[3])
+    complete(layers[3])
     layer_sum.forward(0)
     layer_sum.wait_terms(0)
     copies.arrived(tgt.at[other_core], near + 2, partner)
@@ -560,7 +588,6 @@
 
     err_gather = ColGather(copies, err)
     err_gather.start()
-    err_gather.run()
 
     back_sum = RowSum(copies, 2, back, back_landed, back_pair, back_pair_landed)
 
@@ -575,13 +602,11 @@
             back[place, 0, index] = whole[:, :LANES]
             back[place, 1, index] = whole[:, LANES:]
 
-    turn_back(x_opposite)
-    each(2, back_sum.ring.send_opposite)
-    turn_back(x_plus)
-    each(2, back_sum.ring.send_plus)
-    turn_back(x_minus)
-    each(2, back_sum.ring.send_minus)
-    turn_back(x_here)
+    def turn_back_and_send(place):
+        turn_back(place)
+        each(2, lambda index: back_sum.ring.send_for(place, index))
+
+    err_gather.run(turn_back_and_send)
     each(2, back_sum.ring.forward)
     each(2, back_sum.pair)
     each(2, lambda index: back_sum.finish(d_hid.at[index], index))
@@ -628,21 +653,24 @@
     copies.send(grads_down.at[other_core], grads_down_landed, near + 4, partner)
     down_grads(core)
 
-    each(4, pre_gather.finish)
-
-    def pre_grads(side):
+    def tokens_of(place, side):
+        return x[place, :, side].reshape(RING * HALF, FEATS)
+
+    def first_grads(side):
         def one(index):
-            total = jnp.zeros((PADDED, FEATS), F32)
-            for place in range(RING):
-                tokens_block = x[place, :, side].reshape(RING * HALF, FEATS)
-                total = total + dot_nn(whole_units(d_pre, place, index), tokens_block)
+            total = dot_nn(whole_units(d_pre, x_here, index), tokens_of(x_here, side))
+            for place in (x_minus, x_plus):
+                total = total + dot_nn(whole_units(d_pre, place, index), tokens_of(place, side))
             grads[side, index] = total
 
         each(4, one)
 
-    pre_grads(other_core)
-    copies.send(grads.at[other_core], grads_landed, near + 5, partner)
-    pre_grads(core)
+    def last_grads(side, index):
+        last = dot_nn(whole_units(d_pre, x_opposite, index), tokens_of(x_opposite, side))
+        grads[side, index] = grads[side, index] + last
+
+    first_grads(other_core)
+    first_grads(core)
 
     def squares(values):
         return jnp.sum(values * values, axis=0, keepdims=True)
@@ -656,22 +684,25 @@
     curv_down_out[...] = curv[:UNITS]
     curv_sum = squares(curv)
 
-    tall[PADDED - 32 :] = jnp.zeros((3 * LANES - PADDED + 32, FEATS), F32)
-
-    def turned(values, out):
-        tall[:PADDED] = values
-        out[...] = tall[...].T[:, :UNITS]
-
-    copies.arrived(grads_landed, near + 5, partner)
+    def last_and_send(index):
+        pre_gather.finish(index)
+        last_grads(other_core, index)
+        copies.send(grads.at[other_core, index], grads_landed.at[index], near + 5 + index, partner)
+
+    each(4, last_and_send)
+    each(4, lambda index: last_grads(core, index))
+
     for index, (grad_out, curv_out) in enumerate(
         ((grad_gate_out, curv_gate_out), (grad_up_out, curv_up_out))
     ):
+        copies.arrived(grads_landed.at[index], near + 5 + index, partner)
         grad = grads[core, index] + grads_landed[index]
-        turned(grad, grad_out)
+        grad_out[...] = grad[:UNITS]
         grad_sum = grad_sum + squares(grad)
+        copies.arrived(grads_landed.at[2 + index], near + 7 + index, partner)
         hess = grads[core, 2 + index] + grads_landed[2 + index]
         curv = curvature(proj[core, 2 + index].astype(F32), hess)
-        turned(curv, curv_out)
+        curv_out[...] = curv[:UNITS]
         curv_sum = curv_sum + squares(curv)
 
     lane = lax.broadcasted_iota(jnp.int32, (8, LANES), 1)
@@ -703,7 +734,7 @@
     copies.sent(tgt.at[0], near + 2, partner)
     copies.sent(down.at[0], near + 3, partner)
     copies.sent(grads_down_landed, near + 4, partner)
-    copies.sent(grads_landed, near + 5, partner)
+    each(4, lambda index: copies.sent(grads_landed.at[index], near + 5 + index, partner))
     x_gather.drain()
     err_gather.drain()
     each(4, row_sum.drain)
@@ -722,26 +753,17 @@
 
 
 def whole_step(*operands):
-    natural = jax.ShapeDtypeStruct((FEATS, UNITS), F32)
-    turned = jax.ShapeDtypeStruct((UNITS, FEATS), F32)
     units = (PADDED, LANES)
     block = (2, HALF, FEATS)
     return pl.pallas_call(
         step_kernel,
         out_shape=(
-            natural,
-            natural,
-            turned,
-            natural,
-            natural,
-            turned,
+            *[jax.ShapeDtypeStruct((UNITS, FEATS), F32)] * 6,
             jax.ShapeDtypeStruct((8, LANES), F32),
         ),
         in_specs=[pl.BlockSpec(memory_space=pltpu.VMEM)] * 8,
         out_specs=[pl.BlockSpec(memory_space=pltpu.VMEM)] * 7,
         scratch_shapes=[
-            pltpu.VMEM((FEATS, 3 * LANES), BF16),
-            pltpu.VMEM((3 * LANES, FEATS), F32),
             pltpu.VMEM((2, 4, PADDED, FEATS), BF16),
             pltpu.VMEM((2, 2, PADDED, FEATS), BF16),
             pltpu.VMEM((RING, RING, *block), BF16),
@@ -796,7 +818,7 @@
     second_down,
 ):
     grad_gate, grad_up, grad_down, curv_gate, curv_up, curv_down, sums = whole_step(
-        tokens, target, gate_weight, up_weight, down_weight, probe_gate, probe_up, probe_down
+        tokens, target, gate_weight.T, up_weight.T, down_weight, probe_gate.T, probe_up.T, probe_down
     )
     count = 3.0 * D * FF
     rms_grad = jnp.sqrt(sums[0, 0] / count + 1e-06)
@@ -807,8 +829,8 @@
     seconds = []
     updates = []
     for grad, curv, first, second in (
-        (grad_gate, curv_gate, first_gate, second_gate),
-        (grad_up, curv_up, first_up, second_up),
+        (grad_gate, curv_gate, first_gate.T, second_gate.T),
+        (grad_up, curv_up, first_up.T, second_up.T),
         (grad_down, curv_down, first_down, second_down),
     ):
         new_first = 0.9 * first + 0.1 * (grad / rms_grad)
@@ -817,7 +839,8 @@
         firsts.append(new_first)
         seconds.append(new_second)
         updates.append(new_first / fix_first / (jnp.sqrt(new_second / fix_second) + 1e-08))
-    return (*firsts, *seconds, *updates)
+    outs = (firsts, seconds, updates)
+    return tuple(value for gate, up, down in outs for value in (gate.T, up.T, down))
 
 
 def solution(mesh):

time: 194 us -> 178 us (0.918)
  local copies, waits for them, and re-layouts: 15.4 us -> 1.38 us
  Pallas kernels: 173 us -> 169 us
    unnamed x36 -> x16, local copies, waits for them, and re-layouts: 14.1 us -> 0.04 us
    pallas_call x1, Pallas kernels: 173 us -> 169 us  [whole_step(): pl.pallas_call(step_kernel, out_shape=(*[jax.ShapeDtypeStruct((UNITS, FEA...]
where the time goes in v3:
time: 178 us; the launch traced here: 177 us
  Pallas kernels  169 us (95%)
  other arithmetic  4.11 us (2%)
  between operations  2.16 us (1%)
    pallas_call x1, Pallas kernels, whole_step(): pl.pallas_call(step_kernel, out_shape=(*[jax.ShapeDtypeStruct((UNITS, FEA...  169 us

profile of v3, /device:TPU:32, one launch (start us, length us, event | category | flops | bytes accessed | tf_op | source)
XLA Modules:
  0.0 177.0 jit_solution(1957994658324136149)
XLA Ops:
  0.6 0.0 copy-start.4
  0.7 0.0 copy-start.5
  0.7 0.0 copy-start.6
  0.7 0.0 copy-start.7
  0.7 169.3 %shard_map.205 = (f32[344,256]{1,0:T(8,128)}, f32[344,256]{1,0:T(8,128)}, f32[344,256]{1,0:T(8,128)}, f32[344,256]{1,0:T(8,128)}, f32[344,256]{1,0:T(8,128)}, /*index=5*/f32[344,256]{1,0:T(8,128)}, f32[8,128]{1,0:T(8,128)}) custom-call(bf16[128,256]{1,0:T(8,128)(2,1)} %tokens.1, bf16[128,256]{1,0:T(8,128)(2,1)} %target.1, bf16[344,256]{1,0:T(8,128)(2,1)} %bitcast.44, ...), custom_call_target="tpu_custom_call" | custom-call | tf_op jit(solution)/shard_map/pallas_call | solution.py:758
  170.0 1.3 fusion.4
  172.8 0.0 copy-done.4
  172.8 0.0 copy-done.5
  172.8 0.0 copy-done.6
  172.8 0.0 copy-done.7
  172.8 0.0 copy-start
  172.8 0.0 copy-start.1
  172.8 0.0 copy-start.2
  172.8 0.0 copy-start.3
  172.8 3.0 %add_divide_fusion = (f32[344,256]{1,0:T(8,128)}, f32[344,256]{1,0:T(8,128)}, f32[344,256]{1,0:T(8,128)}, f32[256,344]{0,1:T(8,128)}, f32[256,344]{0,1:T(8,128)}, /*index=5*/f32[256,344]{0,1:T(8,128)}) fusion(f32[344,256]{1,0:T(8,128)} %get-tuple-element.22, f32[]{:T(128)} %bitcast.10, f32[344,256]{1,0:T(8,128)S(1)} %copy-done.4, ...), kind=kLoop, calls=%fused_computation.4 | loop fusion | flops 2289664 | bytes 4931592 | tf_op jit(solution)/shard_map/div | solution.py:841
  175.9 0.0 copy-done
  175.9 0.0 copy-done.1
  175.9 0.0 copy-done.2
  175.9 0.0 copy-done.3
  175.9 1.1 divide_bitcast_fusion.1
Async XLA Ops:
  0.6 172.1 %copy-start.4 = (f32[344,256]{1,0:T(8,128)S(1)}, f32[344,256]{1,0:T(8,128)}, u32[]{:S(2)}) copy-start(f32[344,256]{1,0:T(8,128)} %param.27) | copy-start | bytes 1056772
  0.7 172.1 %copy-start.5 = (f32[344,256]{1,0:T(8,128)S(1)}, f32[344,256]{1,0:T(8,128)}, u32[]{:S(2)}) copy-start(f32[344,256]{1,0:T(8,128)} %param.24) | copy-start | bytes 1056772
  0.7 172.1 %copy-start.6 = (f32[256,344]{0,1:T(8,128)S(1)}, f32[256,344]{0,1:T(8,128)}, u32[]{:S(2)}) copy-start(f32[256,344]{0,1:T(8,128)} %param.23) | copy-start | bytes 1056772
  0.7 172.1 %copy-start.7 = (f32[256,344]{0,1:T(8,128)S(1)}, f32[256,344]{0,1:T(8,128)}, u32[]{:S(2)}) copy-start(f32[256,344]{0,1:T(8,128)} %param.26) | copy-start | bytes 1056772
  172.8 3.1 %copy-start = (f32[256,344]{0,1:T(8,128)S(1)}, f32[256,344]{0,1:T(8,128)}, u32[]{:S(2)}) copy-start(f32[256,344]{0,1:T(8,128)} %param.22) | copy-start | bytes 1056772
  172.8 3.0 %copy-start.1 = (f32[256,344]{0,1:T(8,128)S(1)}, f32[256,344]{0,1:T(8,128)}, u32[]{:S(2)}) copy-start(f32[256,344]{0,1:T(8,128)} %param.25) | copy-start | bytes 1056772
  172.8 3.0 %copy-start.2 = (f32[344,256]{1,0:T(8,128)S(1)}, f32[344,256]{1,0:T(8,128)}, u32[]{:S(2)}) copy-start(f32[344,256]{1,0:T(8,128)} %get-tuple-element.16) | copy-start | bytes 1056772
  172.8 3.0 %copy-start.3 = (f32[344,256]{1,0:T(8,128)S(1)}, f32[344,256]{1,0:T(8,128)}, u32[]{:S(2)}) copy-start(f32[344,256]{1,0:T(8,128)} %get-tuple-element.20) | copy-start | bytes 1056772

commit v4 on v3

v4 whole, which is shorter than its diff:
```python
import jax
import jax.numpy as jnp
from jax import lax
from jax.experimental import pallas as pl
from jax.experimental.pallas import tpu as pltpu
from jax.sharding import Mesh
from jax.sharding import PartitionSpec as P

D = 4096
FF = 5504
STEP = 10
COL = ("col_0", "col_1")
ROW = ("row_0", "row_1", "row_2")
RING = 4
UNITS = 344
PADDED = 352
FEATS = 256
HALF = 64
LANES = 128
STRIP = 32
MESH = pl.DeviceIdType.MESH
BF16 = jnp.bfloat16
F32 = jnp.float32

X_AXIS, Z_AXIS, CORE_AXIS = ROW
H_AXIS, Y_AXIS = COL


def dot_nn(left, right):
    return jnp.dot(left, right, preferred_element_type=F32)


def dot_nt(left, right):
    return lax.dot_general(left, right, (((1,), (1,)), ((), ())), preferred_element_type=F32)


def dot_tn(left, right):
    return lax.dot_general(left, right, (((0,), (0,)), ((), ())), preferred_element_type=F32)


def block_ones(size):
    rows = lax.broadcasted_iota(jnp.int32, (size, size), 0) >> 2
    cols = lax.broadcasted_iota(jnp.int32, (size, size), 1) >> 2
    return jnp.where(rows == cols, 1.0, 0.0).astype(BF16)


def two_terms(values):
    high = values.astype(BF16)
    low = (values - high.astype(F32)).astype(BF16)
    return high, low


def curvature(sign, hess):
    high, low = two_terms(jnp.abs(sign * hess))
    ones = block_ones(hess.shape[0])
    down = dot_nn(ones, high) + dot_nn(ones, low)
    high, low = two_terms(down)
    ones = block_ones(hess.shape[1])
    return (dot_nn(high, ones) + dot_nn(low, ones)) * 0.0625


class Copies:
    def __init__(self, send_sems, recv_sems):
        self.send_sems = send_sems
        self.recv_sems = recv_sems
        self.next_in = 0
        self.next_out = 0

    def slots(self, count):
        self.next_in += count
        return self.next_in - count

    def outs(self, count):
        self.next_out += count
        return self.next_out - count

    def copy(self, src, dst, out, slot, peer):
        return pltpu.make_async_remote_copy(
            src_ref=src,
            dst_ref=dst,
            send_sem=self.send_sems.at[out],
            recv_sem=self.recv_sems.at[slot],
            device_id=peer,
            device_id_type=MESH,
        )

    def send(self, src, dst, out, slot, peer):
        self.copy(src, dst, out, slot, peer).start()

    def arrived(self, dst, slot, peer):
        self.copy(dst, dst, 0, slot, peer).wait_recv()

    def sent(self, src, out, peer):
        self.copy(src, src, out, 0, peer).wait_send()


def around(axis):
    here = lax.axis_index(axis)
    return here, lax.rem(here + 1, RING), lax.rem(here + 3, RING), lax.rem(here + 2, RING)


def add_strips(dst, terms):
    def strip(index, carry):
        rows = pl.ds(pl.multiple_of(index * STRIP, STRIP), STRIP)
        total = terms[0][rows, :].astype(F32)
        for term in terms[1:]:
            total = total + term[rows, :].astype(F32)
        dst[rows, :] = total.astype(dst.dtype)
        return carry

    lax.fori_loop(0, PADDED // STRIP, strip, 0)


def add_blocks(dst, terms):
    total = terms[0][...].astype(F32)
    for term in terms[1:]:
        total = total + term[...].astype(F32)
    dst[...] = total.astype(dst.dtype)


class RingSum:
    def __init__(self, copies, axis, count, block, landed, all_landed, number=lambda index: index):
        self.number, self.all_landed = number, all_landed
        self.out = copies.outs(6)
        self.copies, self.axis, self.block, self.landed = copies, axis, block, landed
        self.base = copies.slots(6 * count)
        self.count = count
        self.here, self.plus, self.minus, self.opposite = around(axis)

    def slot(self, kind, index):
        return self.base + kind * self.count + self.number(index)

    def send(self, src, kind, index, peer):
        slot = self.slot(kind, index)
        self.copies.send(src, self.landed(kind, index), self.out + kind, slot, {self.axis: peer})

    def wait(self, kind, index):
        ref = self.landed(kind, index)
        self.copies.arrived(ref, self.slot(kind, index), {self.axis: self.plus})

    def send_for(self, place, index):
        role = lax.rem(place - self.here + RING, RING)

        @pl.when(role == 1)
        def _():
            self.send(self.block(place, 1, index), 3, index, self.plus)

        @pl.when(role == 2)
        def _():
            self.send(self.block(place, 0, index), 0, index, self.plus)
            self.send(self.block(place, 1, index), 1, index, self.minus)

        @pl.when(role == 3)
        def _():
            self.send(self.block(place, 0, index), 4, index, self.minus)

    def send_opposite(self, index):
        self.send(self.block(self.opposite, 0, index), 0, index, self.plus)
        self.send(self.block(self.opposite, 1, index), 1, index, self.minus)

    def send_plus(self, index):
        self.send(self.block(self.plus, 1, index), 3, index, self.plus)

    def send_minus(self, index):
        self.send(self.block(self.minus, 0, index), 4, index, self.minus)

    def forward(self, index):
        self.wait(0, index)
        ref = self.block(self.plus, 0, index)
        add_blocks(ref, (ref, self.landed(0, index)))
        self.send(ref, 2, index, self.plus)
        self.wait(1, index)
        ref = self.block(self.minus, 1, index)
        add_blocks(ref, (ref, self.landed(1, index)))
        self.send(ref, 5, index, self.minus)

    def wait_terms(self, index):
        for kind in (3, 4, 2, 5):
            self.wait(kind, index)

    def terms(self, half, index):
        return (
            self.block(self.here, half, index),
            self.landed(2 + half, index),
            self.landed(4 + half, index),
        )

    def drain(self):
        for kind in range(6):
            self.copies.sent(self.all_landed(kind), self.out + kind, {self.axis: self.plus})


class RowSum:
    def __init__(self, copies, count, blocks, landed):
        self.copies, self.count, self.blocks, self.landed = copies, count, blocks, landed
        self.base, self.out = copies.slots(7 * count), copies.outs(7)
        self.here, self.plus, self.minus, self.opposite = around(X_AXIS)
        self.z = lax.axis_index(Z_AXIS)
        self.other = 1 - self.z

    def send(self, place, half, kind, index, peer):
        slot = self.base + kind * self.count + index
        src = self.blocks.at[place, half, index]
        self.copies.send(src, self.landed.at[kind, index], self.out + kind, slot, peer)

    def wait(self, kind, index):
        slot = self.base + kind * self.count + index
        self.copies.arrived(self.landed.at[kind, index], slot, {Z_AXIS: self.other})

    def send_for(self, place, index):
        role = lax.rem(place - self.here + RING, RING)

        @pl.when(role == 1)
        def _():
            self.send(place, 1, 3, index, {X_AXIS: self.plus})

        @pl.when(role == 2)
        def _():
            self.send(place, 0, 0, index, {X_AXIS: self.plus})
            self.send(place, 1, 1, index, {X_AXIS: self.minus})

        @pl.when(role == 3)
        def _():
            self.send(place, 0, 4, index, {X_AXIS: self.minus})

    def forward(self, index):
        self.wait(0, index)
        ref = self.blocks.at[self.plus, 0, index]
        add_strips(ref, (ref, self.landed.at[0, index]))
        self.send(self.plus, 0, 2, index, {X_AXIS: self.plus})
        self.wait(1, index)
        ref = self.blocks.at[self.minus, 1, index]
        add_strips(ref, (ref, self.landed.at[1, index]))
        self.send(self.minus, 1, 5, index, {X_AXIS: self.minus})

    def terms(self, half, index):
        return (
            self.blocks.at[self.here, half, index],
            self.landed.at[2 + half, index],
            self.landed.at[4 + half, index],
        )

    def pair(self, index):
        for kind in (3, 4, 2, 5):
            self.wait(kind, index)
        add_strips(self.blocks.at[self.here, self.other, index], self.terms(self.other, index))
        self.send(self.here, self.other, 6, index, {Z_AXIS: self.other})

    def finish(self, dst, index):
        self.wait(6, index)
        add_strips(dst, (*self.terms(self.z, index), self.landed.at[6, index]))

    def drain(self):
        for kind in range(7):
            self.copies.sent(self.landed.at[kind], self.out + kind, {Z_AXIS: self.other})


class RowGather:
    def __init__(self, copies, count, buffer):
        self.copies, self.count, self.buffer = copies, count, buffer
        self.base, self.out = copies.slots(7 * count), copies.outs(7)
        self.here, self.plus, self.minus, self.opposite = around(X_AXIS)
        self.z = lax.axis_index(Z_AXIS)
        self.other = 1 - self.z

    def send(self, place, z, kind, index, peer):
        ref = self.buffer.at[place, z, index]
        slot = self.base + kind * self.count + index
        self.copies.send(ref, ref, self.out + kind, slot, peer)

    def wait(self, place, z, kind, index):
        ref = self.buffer.at[place, z, index]
        slot = self.base + kind * self.count + index
        self.copies.arrived(ref, slot, {Z_AXIS: self.other})

    def start(self, index):
        self.send(self.here, self.z, 0, index, {Z_AXIS: self.other})
        self.send(self.here, self.z, 1, index, {X_AXIS: self.plus})
        self.send(self.here, self.z, 2, index, {X_AXIS: self.minus})

    def pair(self, index):
        self.wait(self.here, self.other, 0, index)
        self.send(self.here, self.other, 3, index, {X_AXIS: self.plus})
        self.send(self.here, self.other, 4, index, {X_AXIS: self.minus})

    def forward(self, index):
        self.wait(self.minus, self.z, 1, index)
        self.wait(self.minus, self.other, 3, index)
        self.send(self.minus, 0, 5, index, {X_AXIS: self.plus})
        self.wait(self.plus, self.z, 2, index)
        self.wait(self.plus, self.other, 4, index)
        self.send(self.plus, 1, 6, index, {X_AXIS: self.minus})

    def finish(self, index):
        self.wait(self.opposite, 0, 5, index)
        self.wait(self.opposite, 1, 6, index)

    def drain(self):
        for kind in range(7):
            self.copies.sent(self.buffer.at[0, 0], self.out + kind, {Z_AXIS: self.other})


class RingGather:
    def __init__(self, copies, axis, whole, half, out):
        self.copies, self.axis, self.whole, self.half = copies, axis, whole, half
        self.base, self.out = copies.slots(4), out
        self.here, self.plus, self.minus, self.opposite = around(axis)

    def send(self, ref, kind, peer):
        self.copies.send(ref, ref, self.out + kind, self.base + kind, {self.axis: peer})

    def wait(self, ref, kind):
        self.copies.arrived(ref, self.base + kind, {self.axis: self.plus})

    def start(self):
        self.send(self.whole(self.here), 0, self.plus)
        self.send(self.whole(self.here), 1, self.minus)

    def from_minus(self):
        self.wait(self.whole(self.minus), 0)
        self.send(self.half(self.minus, 0), 2, self.plus)

    def from_plus(self):
        self.wait(self.whole(self.plus), 1)
        self.send(self.half(self.plus, 1), 3, self.minus)

    def forward(self):
        self.from_minus()
        self.from_plus()

    def finish(self):
        self.wait(self.half(self.opposite, 0), 2)
        self.wait(self.half(self.opposite, 1), 3)


class ColGather:
    def __init__(self, copies, buffer):
        here, plus, minus, opposite = around(H_AXIS)
        y = lax.axis_index(Y_AXIS)
        self.copies, self.buffer = copies, buffer
        self.out = copies.outs(8)
        self.outer = RingGather(
            copies,
            H_AXIS,
            lambda place: buffer.at[place, y],
            lambda place, half: buffer.at[place, y, half],
            self.out,
        )
        self.inner = [
            RingGather(
                copies,
                Y_AXIS,
                lambda place, layer=layer: buffer.at[layer, place],
                lambda place, half, layer=layer: buffer.at[layer, place, half],
                self.out + 4,
            )
            for layer in (here, minus, plus, opposite)
        ]
        self.places = (here, minus, plus, opposite)

    def start(self):
        self.outer.start()
        self.inner[0].start()

    def spread(self):
        self.inner[0].forward()

    def outward(self):
        self.outer.from_minus()
        self.inner[1].start()
        self.outer.from_plus()
        self.inner[2].start()

    def first(self, use):
        self.inner[0].finish()
        use(self.places[0])

    def middle(self):
        self.inner[1].forward()
        self.inner[2].forward()
        self.outer.finish()
        self.inner[3].start()

    def second(self, use):
        self.inner[1].finish()
        use(self.places[1])
        self.inner[2].finish()
        use(self.places[2])
        self.inner[3].forward()

    def last(self, use):
        self.inner[3].finish()
        use(self.places[3])

    def drain(self):
        for kind in range(4):
            one = self.buffer.at[0, 0] if kind < 2 else self.buffer.at[0, 0, 0]
            all_layers = self.buffer.at[0] if kind < 2 else self.buffer.at[0, pl.ds(0, 2)]
            self.copies.sent(one, self.out + kind, {H_AXIS: self.outer.plus})
            self.copies.sent(all_layers, self.out + 4 + kind, {H_AXIS: self.outer.plus})


def step_kernel(
    tokens,
    target,
    gate_weight,
    up_weight,
    down_weight,
    probe_gate,
    probe_up,
    probe_down,
    grad_gate_out,
    grad_up_out,
    grad_down_out,
    curv_gate_out,
    curv_up_out,
    curv_down_out,
    sums_out,
    proj,
    down,
    x,
    tgt,
    part,
    part_landed,
    pre,
    hid,
    outs,
    outs_landed,
    layer_sums,
    layer_landed,
    final,
    err,
    back,
    back_landed,
    d_hid,
    coef,
    d_pre,
    grads,
    grads_landed,
    grads_down,
    grads_down_landed,
    tiles,
    tiles_landed,
    results,
    send_sems,
    recv_sems,
    out_sems,
):
    copies = Copies(send_sems, recv_sems)
    core = lax.axis_index(CORE_AXIS)
    other_core = 1 - core
    x_here, x_plus, x_minus, x_opposite = around(X_AXIS)
    y_here, y_plus, y_minus, y_opposite = around(Y_AXIS)
    h_here, h_plus, h_minus, h_opposite = around(H_AXIS)
    z_here = lax.axis_index(Z_AXIS)
    partner = {CORE_AXIS: other_core}

    barrier = pltpu.get_barrier_semaphore()
    z_other = 1 - z_here
    peers = [partner, {Z_AXIS: z_other}]
    for axis in (X_AXIS, Y_AXIS, H_AXIS):
        peers += [{axis: place} for place in around(axis)[1:]]
    for peer in peers:
        pl.semaphore_signal(barrier, inc=1, device_id=peer, device_id_type=MESH)

    own_rows = pl.ds(pl.multiple_of(core * HALF, HALF), HALF)
    other_rows = pl.ds(pl.multiple_of(other_core * HALF, HALF), HALF)
    x[h_here, y_here, core] = tokens[own_rows, :]
    tgt[core] = target[own_rows, :]

    def sign(ref):
        return (2 * ref[...] - 1).astype(F32).astype(BF16)

    def lay_out(dst, index, values):
        dst[core, index, PADDED - 32 :] = jnp.zeros((32, FEATS), BF16)
        dst[core, index, :UNITS] = values

    lay_out(proj, 0, gate_weight[...])
    lay_out(proj, 1, up_weight[...])
    lay_out(proj, 2, sign(probe_gate))
    lay_out(proj, 3, sign(probe_up))
    lay_out(down, 0, down_weight[...])
    lay_out(down, 1, sign(probe_down))

    pl.semaphore_wait(barrier, len(peers))
    near = copies.slots(9)
    copies.outs(9)
    copies.send(tokens.at[other_rows], x.at[h_here, y_here, core], near, near, partner)
    copies.send(proj.at[core], proj.at[core], near + 1, near + 1, partner)
    copies.send(target.at[other_rows], tgt.at[core], near + 2, near + 2, partner)
    copies.send(down.at[core], down.at[core], near + 3, near + 3, partner)

    copies.arrived(x.at[h_here, y_here, other_core], near, partner)
    x_gather = ColGather(copies, x)
    x_gather.start()
    x_gather.spread()
    x_gather.outward()

    def token_block(ref, *place):
        return [
            ref[(*place, slice(None), half)].reshape(RING * HALF, FEATS) for half in range(2)
        ]

    row_sum = RowSum(copies, 4, part, part_landed)

    def project(index, place):
        left, right = token_block(x, place)
        both = dot_nt(proj[0, index], left) + dot_nt(proj[1, index], right)
        both = both.astype(BF16)
        part[place, 0, index] = both[:, :LANES]
        part[place, 1, index] = both[:, LANES:]

    def each(count, step):
        def body(index, carry):
            step(index)
            return carry

        lax.fori_loop(0, count, body, 0)

    def project_and_send(place):
        def one(index):
            project(index, place)
            row_sum.send_for(place, index)

        each(4, one)

    def project_first(place):
        copies.arrived(proj.at[other_core], near + 1, partner)
        project_and_send(place)

    x_gather.first(project_first)
    x_gather.middle()
    x_gather.second(project_and_send)
    x_gather.last(project_and_send)
    each(4, row_sum.forward)
    each(4, row_sum.pair)

    def strips(step):
        def body(index, carry):
            step(pl.ds(pl.multiple_of(index * STRIP, STRIP), STRIP))
            return carry

        lax.fori_loop(0, PADDED // STRIP, body, 0)

    def hide(rows):
        pre_gate, pre_up = pre[0, rows, :], pre[1, rows, :]
        act = pre_gate * jax.nn.sigmoid(pre_gate)
        hid[x_here, z_here, 0, rows, :] = (act * pre_up).astype(BF16)

    def hide_dot(rows):
        pre_gate, pre_up = pre[0, rows, :], pre[1, rows, :]
        dot_gate, dot_up = pre[2, rows, :], pre[3, rows, :]
        sig = jax.nn.sigmoid(pre_gate)
        act = pre_gate * sig
        slope = sig * (1.0 + pre_gate * (1.0 - sig))
        bend = sig * (1.0 - sig) * (2.0 + pre_gate * (1.0 - 2.0 * sig))
        hid[x_here, z_here, 1, rows, :] = (slope * dot_gate * pre_up + act * dot_up).astype(BF16)
        coef[x_here, z_here, 0, rows, :] = (pre_up * slope).astype(BF16)
        coef[x_here, z_here, 1, rows, :] = act.astype(BF16)
        coef[x_here, z_here, 2, rows, :] = (dot_up * slope + pre_up * bend * dot_gate).astype(BF16)
        coef[x_here, z_here, 3, rows, :] = (slope * dot_gate).astype(BF16)

    hid_gather = RowGather(copies, 2, hid)
    each(2, lambda index: row_sum.finish(pre.at[index], index))
    strips(hide)
    hid_gather.start(0)
    each(2, lambda index: row_sum.finish(pre.at[2 + index], 2 + index))
    strips(hide_dot)
    hid_gather.start(1)
    layers = [(0, x_here), (1, x_minus), (2, x_plus), (3, x_opposite)]

    def out_ring(stream):
        return RingSum(
            copies,
            Y_AXIS,
            4,
            lambda place, half, layer: outs.at[stream, layer[1], place, half],
            lambda kind, layer: outs_landed.at[stream, kind, layer[0]],
            lambda kind: outs_landed.at[stream, kind],
            lambda layer: layer[0],
        )

    def layer_ring(stream):
        return RingSum(
            copies,
            H_AXIS,
            1,
            lambda place, half, index: layer_sums.at[stream, place, half],
            lambda kind, index: layer_landed.at[stream, kind],
            lambda kind: layer_landed.at[stream, kind],
        )

    out_sums = (out_ring(0), out_ring(1))
    layer_rings = (layer_ring(0), layer_ring(1))
    err_gathers = (ColGather(copies, err.at[0]), ColGather(copies, err.at[1]))
    back_sum = RowSum(copies, 2, back, back_landed)
    coef_gather = RowGather(copies, 4, coef)
    back_gather = RowGather(copies, 2, d_hid)

    def whole_units(ref, place, index):
        return jnp.concatenate([ref[place, 0, index], ref[place, 1, index]], axis=1)

    def expand(stream, layer):
        place = layer[1]
        plain = whole_units(hid, place, 0)
        for half in range(2):
            if stream == 0:
                value = dot_tn(plain, down[half, 0])
            else:
                tangent = whole_units(hid, place, 1)
                value = dot_tn(tangent, down[half, 0]) + dot_tn(plain, down[half, 1])
            value = value.astype(BF16).reshape(RING, HALF, FEATS)
            for block in range(RING):
                outs[stream, place, block, half] = value[block]
        out_sums[stream].send_opposite(layer)
        out_sums[stream].send_plus(layer)
        out_sums[stream].send_minus(layer)

    def complete(stream, layer):
        out_sum = out_sums[stream]
        out_sum.wait_terms(layer)
        for half in range(2):
            add_blocks(layer_sums.at[stream, layer[1], half], out_sum.terms(half, layer))
        layer_rings[stream].send_for(layer[1], 0)

    def settle(stream):
        ring = layer_rings[stream]
        ring.wait_terms(0)
        for half in range(2):
            add_blocks(final.at[half], ring.terms(half, 0))
            value = final[half]
            if stream == 0:
                value = value - tgt[half].astype(F32)
            err[stream, h_here, y_here, half] = value.astype(BF16)
        err_gathers[stream].start()

    def turn_back(stream):
        def one(place):
            plain = token_block(err, 0, place)
            if stream == 0:
                whole = dot_nt(down[0, 0], plain[0]) + dot_nt(down[1, 0], plain[1])
            else:
                tangent = token_block(err, 1, place)
                whole = dot_nt(down[0, 0], tangent[0]) + dot_nt(down[1, 0], tangent[1])
                whole = whole + dot_nt(down[0, 1], plain[0]) + dot_nt(down[1, 1], plain[1])
            whole = whole.astype(BF16)
            back[place, 0, stream] = whole[:, :LANES]
            back[place, 1, stream] = whole[:, LANES:]
            back_sum.send_for(place, stream)

        return one

    def slopes(place):
        for z in range(2):

            def one(rows):
                d_hidden = d_hid[place, z, 0, rows, :].astype(F32)
                for index in range(2):
                    factor = coef[place, z, index, rows, :].astype(F32)
                    d_pre[place, z, index, rows, :] = (d_hidden * factor).astype(BF16)

            strips(one)

    def bends(place):
        for z in range(2):

            def one(rows):
                d_hidden = d_hid[place, z, 0, rows, :].astype(F32)
                d_hidden_dot = d_hid[place, z, 1, rows, :].astype(F32)
                for index in range(2):
                    factor = coef[place, z, index, rows, :].astype(F32)
                    bent = coef[place, z, 2 + index, rows, :].astype(F32)
                    value = d_hidden_dot * factor + d_hidden * bent
                    d_pre[place, z, 2 + index, rows, :] = value.astype(BF16)

            strips(one)

    hid_gather.pair(0)
    copies.arrived(down.at[other_core], near + 3, partner)
    expand(0, layers[0])
    hid_gather.forward(0)
    expand(0, layers[1])
    expand(0, layers[2])
    hid_gather.pair(1)
    expand(1, layers[0])
    out_sums[0].forward(layers[0])
    hid_gather.forward(1)
    expand(1, layers[1])
    expand(1, layers[2])
    each(4, coef_gather.start)
    hid_gather.finish(0)
    expand(0, layers[3])
    complete(0, layers[0])
    out_sums[0].forward(layers[1])
    out_sums[0].forward(layers[2])
    out_sums[1].forward(layers[0])
    hid_gather.finish(1)
    expand(1, layers[3])
    out_sums[0].forward(layers[3])
    complete(0, layers[1])
    complete(0, layers[2])
    complete(1, layers[0])
    out_sums[1].forward(layers[1])
    out_sums[1].forward(layers[2])
    complete(0, layers[3])
    each(4, coef_gather.pair)
    layer_rings[0].forward(0)
    out_sums[1].forward(layers[3])
    complete(1, layers[1])
    complete(1, layers[2])
    copies.arrived(tgt.at[other_core], near + 2, partner)
    settle(0)
    complete(1, layers[3])
    layer_rings[1].forward(0)
    err_gathers[0].spread()
    err_gathers[0].outward()
    settle(1)
    each(4, coef_gather.forward)
    err_gathers[0].first(turn_back(0))
    err_gathers[0].middle()
    err_gathers[1].spread()
    err_gathers[1].outward()
    err_gathers[0].second(turn_back(0))
    err_gathers[1].first(turn_back(1))
    err_gathers[1].middle()
    err_gathers[0].last(turn_back(0))
    err_gathers[1].second(turn_back(1))
    back_sum.forward(0)
    err_gathers[1].last(turn_back(1))
    back_sum.pair(0)
    back_sum.forward(1)
    back_sum.finish(d_hid.at[x_here, z_here, 0], 0)
    back_gather.start(0)
    back_sum.pair(1)
    back_gather.pair(0)
    back_sum.finish(d_hid.at[x_here, z_here, 1], 1)
    back_gather.start(1)
    back_gather.forward(0)
    back_gather.pair(1)
    each(4, coef_gather.finish)

    def down_grads(side):
        plain_sum = jnp.zeros((PADDED, FEATS), F32)
        along_sum = jnp.zeros((PADDED, FEATS), F32)
        for place in range(RING):
            plain = whole_units(hid, place, 0)
            tangent = whole_units(hid, place, 1)
            err_block = err[0, place, :, side].reshape(RING * HALF, FEATS)
            dot_block = err[1, place, :, side].reshape(RING * HALF, FEATS)
            plain_sum = plain_sum + dot_nn(plain, err_block)
            along_sum = along_sum + dot_nn(tangent, err_block) + dot_nn(plain, dot_block)
        grads_down[side, 0] = plain_sum
        grads_down[side, 1] = along_sum

    down_grads(other_core)
    copies.send(grads_down.at[other_core], grads_down_landed, near + 4, near + 4, partner)
    down_grads(core)

    def tokens_of(place, side):
        return x[place, :, side].reshape(RING * HALF, FEATS)

    def first_grads(side, index):
        total = dot_nn(whole_units(d_pre, x_here, index), tokens_of(x_here, side))
        for place in (x_minus, x_plus):
            total = total + dot_nn(whole_units(d_pre, place, index), tokens_of(place, side))
        grads[side, index] = total

    def last_grads(side, index):
        last = dot_nn(whole_units(d_pre, x_opposite, index), tokens_of(x_opposite, side))
        grads[side, index] = grads[side, index] + last

    def last_and_send(index):
        last_grads(other_core, index)
        copies.send(grads.at[other_core, index], grads_landed.at[index], near + 5 + index, near + 5 + index, partner)
        last_grads(core, index)

    def first_both(index):
        first_grads(other_core, index)
        first_grads(core, index)

    def squares(values):
        return jnp.sum(values * values, axis=0, keepdims=True)

    outputs = (grad_gate_out, grad_up_out, grad_down_out, curv_gate_out, curv_up_out, curv_down_out)

    def to_output(index):
        return pltpu.make_async_copy(results.at[index], outputs[index], out_sems.at[index])

    def give(index, values):
        results[index] = values[:UNITS]
        to_output(index).start()

    for place in (x_here, x_minus, x_plus):
        slopes(place)
    each(2, first_both)
    back_gather.forward(1)
    back_gather.finish(0)
    slopes(x_opposite)
    each(2, last_and_send)
    for place in (x_here, x_minus, x_plus):
        bends(place)
    each(2, lambda index: first_both(2 + index))
    back_gather.finish(1)
    bends(x_opposite)
    each(2, lambda index: last_and_send(2 + index))

    copies.arrived(grads_down_landed, near + 4, partner)
    grad = grads_down[core, 0] + grads_down_landed[0]
    hess = grads_down[core, 1] + grads_down_landed[1]
    give(2, grad)
    grad_sum = squares(grad)
    curv = curvature(down[core, 1].astype(F32), hess)
    give(5, curv)
    curv_sum = squares(curv)

    for index in range(2):
        copies.arrived(grads_landed.at[index], near + 5 + index, partner)
        grad = grads[core, index] + grads_landed[index]
        give(index, grad)
        grad_sum = grad_sum + squares(grad)
    for index in range(2):
        copies.arrived(grads_landed.at[2 + index], near + 7 + index, partner)
        hess = grads[core, 2 + index] + grads_landed[2 + index]
        curv = curvature(proj[core, 2 + index].astype(F32), hess)
        give(3 + index, curv)
        curv_sum = curv_sum + squares(curv)

    lane = lax.broadcasted_iota(jnp.int32, (8, LANES), 1)
    grad_sum = jnp.sum(grad_sum, axis=1, keepdims=True)
    curv_sum = jnp.sum(curv_sum, axis=1, keepdims=True)
    tiles[0] = jnp.where(lane == 0, grad_sum, jnp.where(lane == 1, curv_sum, 0.0))

    stages = [
        [partner],
        [{Z_AXIS: z_other}],
        [{X_AXIS: x_plus}, {X_AXIS: x_opposite}, {X_AXIS: x_minus}],
        [{Y_AXIS: y_plus}, {Y_AXIS: y_opposite}, {Y_AXIS: y_minus}],
        [{H_AXIS: h_plus}, {H_AXIS: h_opposite}, {H_AXIS: h_minus}],
    ]
    small = copies.slots(3 * len(stages))
    small_out = copies.outs(3 * len(stages))
    for stage, receivers in enumerate(stages):
        for index, peer in enumerate(receivers):
            slot = 3 * stage + index
            landed = tiles_landed.at[stage, index]
            copies.send(tiles.at[stage], landed, small_out + slot, small + slot, peer)
        total = tiles[stage]
        for index, peer in enumerate(receivers):
            copies.arrived(tiles_landed.at[stage, index], small + 3 * stage + index, peer)
            total = total + tiles_landed[stage, index]
        tiles[stage + 1] = total
    sums_out[...] = tiles[len(stages)]

    assert (copies.next_out, copies.next_in) == (SENDS, ARRIVALS), (copies.next_out, copies.next_in)
    for index in range(len(outputs)):
        to_output(index).wait()
    copies.sent(x.at[0, 0, 0], near, partner)
    copies.sent(proj.at[0], near + 1, partner)
    copies.sent(tgt.at[0], near + 2, partner)
    copies.sent(down.at[0], near + 3, partner)
    copies.sent(grads_down_landed, near + 4, partner)
    each(4, lambda index: copies.sent(grads_landed.at[index], near + 5 + index, partner))
    x_gather.drain()
    err_gathers[0].drain()
    err_gathers[1].drain()
    row_sum.drain()
    back_sum.drain()
    hid_gather.drain()
    coef_gather.drain()
    back_gather.drain()
    for stream in range(2):
        out_sums[stream].drain()
        layer_rings[stream].drain()
    for stage, receivers in enumerate(stages):
        for index, peer in enumerate(receivers):
            copies.sent(tiles.at[stage], small_out + 3 * stage + index, peer)


SENDS = 107
ARRIVALS = 242


def whole_step(*operands):
    units = (PADDED, LANES)
    block = (2, HALF, FEATS)
    return pl.pallas_call(
        step_kernel,
        out_shape=(
            *[jax.ShapeDtypeStruct((UNITS, FEATS), F32)] * 6,
            jax.ShapeDtypeStruct((8, LANES), F32),
        ),
        in_specs=[pl.BlockSpec(memory_space=pltpu.VMEM)] * 8,
        out_specs=[pl.BlockSpec(memory_space=pl.ANY)] * 6 + [pl.BlockSpec(memory_space=pltpu.VMEM)],
        scratch_shapes=[
            pltpu.VMEM((2, 4, PADDED, FEATS), BF16),
            pltpu.VMEM((2, 2, PADDED, FEATS), BF16),
            pltpu.VMEM((RING, RING, *block), BF16),
            pltpu.VMEM(block, BF16),
            pltpu.VMEM((RING, 2, 4, *units), BF16),
            pltpu.VMEM((7, 4, *units), BF16),
            pltpu.VMEM((4, *units), F32),
            pltpu.VMEM((RING, 2, 2, *units), BF16),
            pltpu.VMEM((2, RING, RING, *block), BF16),
            pltpu.VMEM((2, 6, RING, HALF, FEATS), BF16),
            pltpu.VMEM((2, RING, *block), BF16),
            pltpu.VMEM((2, 6, HALF, FEATS), BF16),
            pltpu.VMEM(block, F32),
            pltpu.VMEM((2, RING, RING, *block), BF16),
            pltpu.VMEM((RING, 2, 2, *units), BF16),
            pltpu.VMEM((7, 2, *units), BF16),
            pltpu.VMEM((RING, 2, 2, *units), BF16),
            pltpu.VMEM((RING, 2, 4, *units), BF16),
            pltpu.VMEM((RING, 2, 4, *units), BF16),
            pltpu.VMEM((2, 4, PADDED, FEATS), F32),
            pltpu.VMEM((4, PADDED, FEATS), F32),
            pltpu.VMEM((2, 2, PADDED, FEATS), F32),
            pltpu.VMEM((2, PADDED, FEATS), F32),
            pltpu.VMEM((6, 8, LANES), F32),
            pltpu.VMEM((5, 3, 8, LANES), F32),
            pltpu.VMEM((6, UNITS, FEATS), F32),
            pltpu.SemaphoreType.DMA((SENDS,)),
            pltpu.SemaphoreType.DMA((ARRIVALS,)),
            pltpu.SemaphoreType.DMA((6,)),
        ],
        compiler_params=pltpu.CompilerParams(
            collective_id=0, has_side_effects=True, vmem_limit_bytes=60 * 1024 * 1024
        ),
    )(*operands)


def update_kernel(sums, *refs):
    count = 3.0 * D * FF
    rms_grad = jnp.sqrt(sums[0:1, 0:1] / count + 1e-06)
    rms_curv = jnp.sqrt(sums[0:1, 1:2] / count + 1e-06)
    fix_first = 1.0 - 0.9**STEP
    fix_second = 1.0 - 0.95**STEP
    for weight in range(3):
        grad, curv, first, second, first_out, second_out, update_out = refs[weight::3]
        new_first = 0.9 * first[...] + 0.1 * (grad[...] / rms_grad)
        scaled = curv[...] / rms_curv
        new_second = 0.95 * second[...] + 0.05 * (scaled * scaled)
        first_out[...] = new_first
        second_out[...] = new_second
        update_out[...] = new_first / fix_first / (jnp.sqrt(new_second / fix_second) + 1e-08)


def update(sums, *arrays):
    rows = pl.BlockSpec((88, FEATS), lambda step: (step, 0))
    return pl.pallas_call(
        update_kernel,
        out_shape=[jax.ShapeDtypeStruct((UNITS, FEATS), F32)] * 9,
        grid=(4,),
        in_specs=[pl.BlockSpec((8, LANES), lambda step: (0, 0))] + [rows] * 12,
        out_specs=[rows] * 9,
    )(sums, *arrays)


def body(
    tokens,
    target,
    gate_weight,
    up_weight,
    down_weight,
    probe_gate,
    probe_up,
    probe_down,
    first_gate,
    first_up,
    first_down,
    second_gate,
    second_up,
    second_down,
):
    *arrays, sums = whole_step(
        tokens, target, gate_weight.T, up_weight.T, down_weight, probe_gate.T, probe_up.T, probe_down
    )
    outs = update(
        sums, *arrays, first_gate.T, first_up.T, first_down, second_gate.T, second_up.T, second_down
    )
    return tuple(value if index % 3 == 2 else value.T for index, value in enumerate(outs))


def solution(mesh):
    torus = Mesh(mesh.devices.reshape(4, 2, 2, 4, 4), (*ROW, *COL))
    feats, units = P(ROW, COL), P(COL, ROW)
    in_specs = (units, units, feats, feats, units) + (feats, feats, units) * 3
    out_specs = (feats, feats, units) * 3
    return jax.shard_map(body, mesh=torus, in_specs=in_specs, out_specs=out_specs, check_vma=False)
```

time: 178 us -> 167 us (0.938)
  other arithmetic: 4.11 us -> 0 us
  Pallas kernels: 169 us -> 166 us
    pallas_call x1, Pallas kernels: 169 us -> 161 us  [whole_step(): pl.pallas_call(step_kernel, out_shape=(*[jax.ShapeDtypeStruct((UNITS, FEA...]
    pallas_call x0 -> x1, Pallas kernels: none -> 5.24 us  [update(): pl.pallas_call(update_kernel, out_shape=[jax.ShapeDtypeStruct((UNITS, FEA...]
    div x1 -> x0, other arithmetic: 3.01 us -> none  [body(): new_first / fix_first / (jnp.sqrt(new_second / fix_second) + 1e-08)]
where the time goes in v4:
time: 167 us
  Pallas kernels  166 us (99%)
    pallas_call x1, Pallas kernels, whole_step(): pl.pallas_call(step_kernel, out_shape=(*[jax.ShapeDtypeStruct((UNITS, FEA...  161 us
    pallas_call x1, Pallas kernels, update(): pl.pallas_call(update_kernel, out_shape=[jax.ShapeDtypeStruct((UNITS, FEA...  5.24 us

profile of v4, /device:TPU:32, one launch (start us, length us, event | category | flops | bytes accessed | tf_op | source)
XLA Modules:
  0.0 166.9 jit_solution(9186218735504449432)
XLA Ops:
  0.6 161.0 %shard_map.205 = (f32[344,256]{1,0:T(8,128)}, f32[344,256]{1,0:T(8,128)}, f32[344,256]{1,0:T(8,128)}, f32[344,256]{1,0:T(8,128)}, f32[344,256]{1,0:T(8,128)}, /*index=5*/f32[344,256]{1,0:T(8,128)}, f32[8,128]{1,0:T(8,128)}) custom-call(bf16[128,256]{1,0:T(8,128)(2,1)} %tokens.1, bf16[128,256]{1,0:T(8,128)(2,1)} %target.1, bf16[344,256]{1,0:T(8,128)(2,1)} %bitcast.20, ...), custom_call_target="tpu_custom_call" | custom-call | tf_op jit(solution)/shard_map/pallas_call | solution.py:886
  161.7 5.2 %shard_map.206 = (f32[344,256]{1,0:T(8,128)}, f32[344,256]{1,0:T(8,128)}, f32[344,256]{1,0:T(8,128)}, f32[344,256]{1,0:T(8,128)}, f32[344,256]{1,0:T(8,128)}, /*...) custom-call(f32[8,128]{1,0:T(8,128)} %get-tuple-element.25.sums, ...), custom_call_target="tpu_custom_call" | custom-call | tf_op jit(solution)/shard_map/pallas_call | solution.py:949

commit v5 on v4

--- a/solution.py
+++ b/solution.py
@@ -119,16 +119,17 @@
 
 
 class RingSum:
-    def __init__(self, copies, axis, count, block, landed, all_landed, number=lambda index: index):
+    def __init__(self, copies, axis, count, block, landed, all_landed, last, number=lambda index: index):
+        self.last = last
         self.number, self.all_landed = number, all_landed
         self.out = copies.outs(6)
         self.copies, self.axis, self.block, self.landed = copies, axis, block, landed
-        self.base = copies.slots(6 * count)
+        self.base = copies.slots(3 * count)
         self.count = count
         self.here, self.plus, self.minus, self.opposite = around(axis)
 
     def slot(self, kind, index):
-        return self.base + kind * self.count + self.number(index)
+        return self.base + min(kind, 2) * self.count + self.number(index)
 
     def send(self, src, kind, index, peer):
         slot = self.slot(kind, index)
@@ -175,8 +176,7 @@
         self.send(ref, 5, index, self.minus)
 
     def wait_terms(self, index):
-        for kind in (3, 4, 2, 5):
-            self.wait(kind, index)
+        self.copies.arrived(self.last(index), self.slot(2, index), {self.axis: self.plus})
 
     def terms(self, half, index):
         return (
@@ -193,19 +193,22 @@
 class RowSum:
     def __init__(self, copies, count, blocks, landed):
         self.copies, self.count, self.blocks, self.landed = copies, count, blocks, landed
-        self.base, self.out = copies.slots(7 * count), copies.outs(7)
+        self.base, self.out = copies.slots(4 * count), copies.outs(7)
         self.here, self.plus, self.minus, self.opposite = around(X_AXIS)
         self.z = lax.axis_index(Z_AXIS)
         self.other = 1 - self.z
 
+    def slot(self, kind, index):
+        return self.base + (0, 1, 2, 2, 2, 2, 3)[kind] * self.count + index
+
     def send(self, place, half, kind, index, peer):
-        slot = self.base + kind * self.count + index
         src = self.blocks.at[place, half, index]
+        slot = self.slot(kind, index)
         self.copies.send(src, self.landed.at[kind, index], self.out + kind, slot, peer)
 
     def wait(self, kind, index):
-        slot = self.base + kind * self.count + index
-        self.copies.arrived(self.landed.at[kind, index], slot, {Z_AXIS: self.other})
+        ref = self.landed.at[pl.ds(2, 4) if kind == 2 else kind, index]
+        self.copies.arrived(ref, self.slot(kind, index), {Z_AXIS: self.other})
 
     def send_for(self, place, index):
         role = lax.rem(place - self.here + RING, RING)
@@ -241,8 +244,7 @@
         )
 
     def pair(self, index):
-        for kind in (3, 4, 2, 5):
-            self.wait(kind, index)
+        self.wait(2, index)
         add_strips(self.blocks.at[self.here, self.other, index], self.terms(self.other, index))
         self.send(self.here, self.other, 6, index, {Z_AXIS: self.other})
 
@@ -274,7 +276,13 @@
         self.copies.arrived(ref, slot, {Z_AXIS: self.other})
 
     def start(self, index):
+        self.start_pair(index)
+        self.start_ring(index)
+
+    def start_pair(self, index):
         self.send(self.here, self.z, 0, index, {Z_AXIS: self.other})
+
+    def start_ring(self, index):
         self.send(self.here, self.z, 1, index, {X_AXIS: self.plus})
         self.send(self.here, self.z, 2, index, {X_AXIS: self.minus})
 
@@ -456,10 +464,21 @@
     partner = {CORE_AXIS: other_core}
 
     barrier = pltpu.get_barrier_semaphore()
-    z_other = 1 - z_here
-    peers = [partner, {Z_AXIS: z_other}]
-    for axis in (X_AXIS, Y_AXIS, H_AXIS):
-        peers += [{axis: place} for place in around(axis)[1:]]
+    def displaced(axes, sizes):
+        steps = [()]
+        for size in sizes:
+            steps = [(*step, more) for step in steps for more in range(size)]
+        return [
+            {
+                axis: lax.rem(lax.axis_index(axis) + more, size)
+                for axis, size, more in zip(axes, sizes, step)
+            }
+            for step in steps[1:]
+        ]
+
+    row_peers = displaced(ROW, (RING, 2, 2))
+    col_peers = displaced(COL, (RING, RING))
+    peers = row_peers + col_peers
     for peer in peers:
         pl.semaphore_signal(barrier, inc=1, device_id=peer, device_id_type=MESH)
 
@@ -555,18 +574,20 @@
         slope = sig * (1.0 + pre_gate * (1.0 - sig))
         bend = sig * (1.0 - sig) * (2.0 + pre_gate * (1.0 - 2.0 * sig))
         hid[x_here, z_here, 1, rows, :] = (slope * dot_gate * pre_up + act * dot_up).astype(BF16)
-        coef[x_here, z_here, 0, rows, :] = (pre_up * slope).astype(BF16)
-        coef[x_here, z_here, 1, rows, :] = act.astype(BF16)
-        coef[x_here, z_here, 2, rows, :] = (dot_up * slope + pre_up * bend * dot_gate).astype(BF16)
-        coef[x_here, z_here, 3, rows, :] = (slope * dot_gate).astype(BF16)
+        coef[x_here, z_here, 0, 0, rows, :] = (pre_up * slope).astype(BF16)
+        coef[x_here, z_here, 0, 1, rows, :] = act.astype(BF16)
+        coef[x_here, z_here, 0, 2, rows, :] = (dot_up * slope + pre_up * bend * dot_gate).astype(BF16)
+        coef[x_here, z_here, 0, 3, rows, :] = (slope * dot_gate).astype(BF16)
 
     hid_gather = RowGather(copies, 2, hid)
+    coef_gather = RowGather(copies, 1, coef)
     each(2, lambda index: row_sum.finish(pre.at[index], index))
     strips(hide)
     hid_gather.start(0)
     each(2, lambda index: row_sum.finish(pre.at[2 + index], 2 + index))
     strips(hide_dot)
     hid_gather.start(1)
+    coef_gather.start_pair(0)
     layers = [(0, x_here), (1, x_minus), (2, x_plus), (3, x_opposite)]
 
     def out_ring(stream):
@@ -577,6 +598,7 @@
             lambda place, half, layer: outs.at[stream, layer[1], place, half],
             lambda kind, layer: outs_landed.at[stream, kind, layer[0]],
             lambda kind: outs_landed.at[stream, kind],
+            lambda layer: outs_landed.at[stream, pl.ds(2, 4), layer[0]],
             lambda layer: layer[0],
         )
 
@@ -588,13 +610,13 @@
             lambda place, half, index: layer_sums.at[stream, place, half],
             lambda kind, index: layer_landed.at[stream, kind],
             lambda kind: layer_landed.at[stream, kind],
+            lambda index: layer_landed.at[stream, pl.ds(2, 4)],
         )
 
     out_sums = (out_ring(0), out_ring(1))
     layer_rings = (layer_ring(0), layer_ring(1))
     err_gathers = (ColGather(copies, err.at[0]), ColGather(copies, err.at[1]))
     back_sum = RowSum(copies, 2, back, back_landed)
-    coef_gather = RowGather(copies, 4, coef)
     back_gather = RowGather(copies, 2, d_hid)
 
     def whole_units(ref, place, index):
@@ -656,7 +678,7 @@
             def one(rows):
                 d_hidden = d_hid[place, z, 0, rows, :].astype(F32)
                 for index in range(2):
-                    factor = coef[place, z, index, rows, :].astype(F32)
+                    factor = coef[place, z, 0, index, rows, :].astype(F32)
                     d_pre[place, z, index, rows, :] = (d_hidden * factor).astype(BF16)
 
             strips(one)
@@ -668,8 +690,8 @@
                 d_hidden = d_hid[place, z, 0, rows, :].astype(F32)
                 d_hidden_dot = d_hid[place, z, 1, rows, :].astype(F32)
                 for index in range(2):
-                    factor = coef[place, z, index, rows, :].astype(F32)
-                    bent = coef[place, z, 2 + index, rows, :].astype(F32)
+                    factor = coef[place, z, 0, index, rows, :].astype(F32)
+                    bent = coef[place, z, 0, 2 + index, rows, :].astype(F32)
                     value = d_hidden_dot * factor + d_hidden * bent
                     d_pre[place, z, 2 + index, rows, :] = value.astype(BF16)
 
@@ -687,7 +709,7 @@
     hid_gather.forward(1)
     expand(1, layers[1])
     expand(1, layers[2])
-    each(4, coef_gather.start)
+    coef_gather.start_ring(0)
     hid_gather.finish(0)
     expand(0, layers[3])
     complete(0, layers[0])
@@ -703,7 +725,7 @@
     out_sums[1].forward(layers[1])
     out_sums[1].forward(layers[2])
     complete(0, layers[3])
-    each(4, coef_gather.pair)
+    coef_gather.pair(0)
     layer_rings[0].forward(0)
     out_sums[1].forward(layers[3])
     complete(1, layers[1])
@@ -715,7 +737,7 @@
     err_gathers[0].spread()
     err_gathers[0].outward()
     settle(1)
-    each(4, coef_gather.forward)
+    coef_gather.forward(0)
     err_gathers[0].first(turn_back(0))
     err_gathers[0].middle()
     err_gathers[1].spread()
@@ -737,7 +759,7 @@
     back_gather.start(1)
     back_gather.forward(0)
     back_gather.pair(1)
-    each(4, coef_gather.finish)
+    coef_gather.finish(0)
 
     def down_grads(side):
         plain_sum = jnp.zeros((PADDED, FEATS), F32)
@@ -830,23 +852,15 @@
     curv_sum = jnp.sum(curv_sum, axis=1, keepdims=True)
     tiles[0] = jnp.where(lane == 0, grad_sum, jnp.where(lane == 1, curv_sum, 0.0))
 
-    stages = [
-        [partner],
-        [{Z_AXIS: z_other}],
-        [{X_AXIS: x_plus}, {X_AXIS: x_opposite}, {X_AXIS: x_minus}],
-        [{Y_AXIS: y_plus}, {Y_AXIS: y_opposite}, {Y_AXIS: y_minus}],
-        [{H_AXIS: h_plus}, {H_AXIS: h_opposite}, {H_AXIS: h_minus}],
-    ]
-    small = copies.slots(3 * len(stages))
-    small_out = copies.outs(3 * len(stages))
+    stages = (row_peers, col_peers)
+    small, small_out = copies.slots(2), copies.outs(2)
     for stage, receivers in enumerate(stages):
         for index, peer in enumerate(receivers):
-            slot = 3 * stage + index
             landed = tiles_landed.at[stage, index]
-            copies.send(tiles.at[stage], landed, small_out + slot, small + slot, peer)
+            copies.send(tiles.at[stage], landed, small_out + stage, small + stage, peer)
+        copies.arrived(tiles_landed.at[stage], small + stage, partner)
         total = tiles[stage]
-        for index, peer in enumerate(receivers):
-            copies.arrived(tiles_landed.at[stage, index], small + 3 * stage + index, peer)
+        for index in range(len(receivers)):
             total = total + tiles_landed[stage, index]
         tiles[stage + 1] = total
     sums_out[...] = tiles[len(stages)]
@@ -871,13 +885,12 @@
     for stream in range(2):
         out_sums[stream].drain()
         layer_rings[stream].drain()
-    for stage, receivers in enumerate(stages):
-        for index, peer in enumerate(receivers):
-            copies.sent(tiles.at[stage], small_out + 3 * stage + index, peer)
-
-
-SENDS = 107
-ARRIVALS = 242
+    for stage in range(2):
+        copies.sent(tiles_landed.at[stage], small_out + stage, partner)
+
+
+SENDS = 94
+ARRIVALS = 160
 
 
 def whole_step(*operands):
@@ -909,14 +922,14 @@
             pltpu.VMEM((RING, 2, 2, *units), BF16),
             pltpu.VMEM((7, 2, *units), BF16),
             pltpu.VMEM((RING, 2, 2, *units), BF16),
-            pltpu.VMEM((RING, 2, 4, *units), BF16),
+            pltpu.VMEM((RING, 2, 1, 4, *units), BF16),
             pltpu.VMEM((RING, 2, 4, *units), BF16),
             pltpu.VMEM((2, 4, PADDED, FEATS), F32),
             pltpu.VMEM((4, PADDED, FEATS), F32),
             pltpu.VMEM((2, 2, PADDED, FEATS), F32),
             pltpu.VMEM((2, PADDED, FEATS), F32),
-            pltpu.VMEM((6, 8, LANES), F32),
-            pltpu.VMEM((5, 3, 8, LANES), F32),
+            pltpu.VMEM((3, 8, LANES), F32),
+            pltpu.VMEM((2, 15, 8, LANES), F32),
             pltpu.VMEM((6, UNITS, FEATS), F32),
             pltpu.SemaphoreType.DMA((SENDS,)),
             pltpu.SemaphoreType.DMA((ARRIVALS,)),
@@ -929,29 +942,54 @@
 
 
 def update_kernel(sums, *refs):
+    given, results = refs[:12], refs[12:21]
+    loaded, computed, load_sems, store_sems = refs[21:]
+    loads = [
+        pltpu.make_async_copy(ref, loaded.at[index], load_sems.at[index])
+        for index, ref in enumerate(given)
+    ]
+    stores = [
+        pltpu.make_async_copy(computed.at[index], ref, store_sems.at[index])
+        for index, ref in enumerate(results)
+    ]
+    for weight in range(3):
+        for load in loads[weight::3]:
+            load.start()
     count = 3.0 * D * FF
     rms_grad = jnp.sqrt(sums[0:1, 0:1] / count + 1e-06)
     rms_curv = jnp.sqrt(sums[0:1, 1:2] / count + 1e-06)
     fix_first = 1.0 - 0.9**STEP
     fix_second = 1.0 - 0.95**STEP
     for weight in range(3):
-        grad, curv, first, second, first_out, second_out, update_out = refs[weight::3]
-        new_first = 0.9 * first[...] + 0.1 * (grad[...] / rms_grad)
-        scaled = curv[...] / rms_curv
-        new_second = 0.95 * second[...] + 0.05 * (scaled * scaled)
-        first_out[...] = new_first
-        second_out[...] = new_second
-        update_out[...] = new_first / fix_first / (jnp.sqrt(new_second / fix_second) + 1e-08)
+        for load in loads[weight::3]:
+            load.wait()
+        grad, curv, first, second = (loaded[index] for index in range(weight, 12, 3))
+        new_first = 0.9 * first + 0.1 * (grad / rms_grad)
+        scaled = curv / rms_curv
+        new_second = 0.95 * second + 0.05 * (scaled * scaled)
+        computed[weight] = new_first
+        computed[3 + weight] = new_second
+        computed[6 + weight] = new_first / fix_first / (jnp.sqrt(new_second / fix_second) + 1e-08)
+        for store in stores[weight::3]:
+            store.start()
+    for store in stores:
+        store.wait()
 
 
 def update(sums, *arrays):
-    rows = pl.BlockSpec((88, FEATS), lambda step: (step, 0))
+    anywhere = pl.BlockSpec(memory_space=pl.ANY)
     return pl.pallas_call(
         update_kernel,
         out_shape=[jax.ShapeDtypeStruct((UNITS, FEATS), F32)] * 9,
-        grid=(4,),
-        in_specs=[pl.BlockSpec((8, LANES), lambda step: (0, 0))] + [rows] * 12,
-        out_specs=[rows] * 9,
+        in_specs=[pl.BlockSpec(memory_space=pltpu.VMEM)] + [anywhere] * 12,
+        out_specs=[anywhere] * 9,
+        scratch_shapes=[
+            pltpu.VMEM((12, UNITS, FEATS), F32),
+            pltpu.VMEM((9, UNITS, FEATS), F32),
+            pltpu.SemaphoreType.DMA((12,)),
+            pltpu.SemaphoreType.DMA((9,)),
+        ],
+        compiler_params=pltpu.CompilerParams(vmem_limit_bytes=62 * 1024 * 1024),
     )(sums, *arrays)
 
 

time: 167 us -> 163 us (0.976)
  Pallas kernels: 166 us -> 161 us
    pallas_call x1, Pallas kernels: 161 us -> 157 us  [whole_step(): pl.pallas_call(step_kernel, out_shape=(*[jax.ShapeDtypeStruct((UNITS, FEA...]
where the time goes in v5:
time: 163 us; the launch traced here: 162 us
  Pallas kernels  161 us (99%)
    pallas_call x1, Pallas kernels, whole_step(): pl.pallas_call(step_kernel, out_shape=(*[jax.ShapeDtypeStruct((UNITS, FEA...  157 us
    pallas_call x1, Pallas kernels, update(): pl.pallas_call(update_kernel, out_shape=[jax.ShapeDtypeStruct((UNITS, FEA...  4.31 us

profile of v5, /device:TPU:32, one launch (start us, length us, event | category | flops | bytes accessed | tf_op | source)
XLA Modules:
  0.0 161.7 jit_solution(3015548696765163619)
XLA Ops:
  0.6 156.8 %shard_map.205 = (f32[344,256]{1,0:T(8,128)}, f32[344,256]{1,0:T(8,128)}, f32[344,256]{1,0:T(8,128)}, f32[344,256]{1,0:T(8,128)}, f32[344,256]{1,0:T(8,128)}, /*index=5*/f32[344,256]{1,0:T(8,128)}, f32[8,128]{1,0:T(8,128)}) custom-call(bf16[128,256]{1,0:T(8,128)(2,1)} %tokens.1, bf16[128,256]{1,0:T(8,128)(2,1)} %target.1, bf16[344,256]{1,0:T(8,128)(2,1)} %bitcast.20, ...), custom_call_target="tpu_custom_call" | custom-call | tf_op jit(solution)/shard_map/pallas_call | solution.py:899
  157.4 4.3 %shard_map.206 = (f32[344,256]{1,0:T(8,128)}, f32[344,256]{1,0:T(8,128)}, f32[344,256]{1,0:T(8,128)}, f32[344,256]{1,0:T(8,128)}, f32[344,256]{1,0:T(8,128)}, /*...) custom-call(f32[8,128]{1,0:T(8,128)} %get-tuple-element.25.sums, ...), custom_call_target="tpu_custom_call" | custom-call | tf_op jit(solution)/shard_map/pallas_call | solution.py:981

commit v6 on v5

--- a/solution.py
+++ b/solution.py
@@ -389,12 +389,15 @@
         self.outer.finish()
         self.inner[3].start()
 
-    def second(self, use):
+    def second(self, use, early):
         self.inner[1].finish()
         use(self.places[1])
+        if early:
+            self.inner[3].forward()
         self.inner[2].finish()
         use(self.places[2])
-        self.inner[3].forward()
+        if not early:
+            self.inner[3].forward()
 
     def last(self, use):
         self.inner[3].finish()
@@ -409,14 +412,14 @@
 
 
 def step_kernel(
-    tokens,
-    target,
-    gate_weight,
-    up_weight,
-    down_weight,
-    probe_gate,
-    probe_up,
-    probe_down,
+    tokens_in,
+    target_in,
+    gate_weight_in,
+    up_weight_in,
+    down_weight_in,
+    probe_gate_in,
+    probe_up_in,
+    probe_down_in,
     grad_gate_out,
     grad_up_out,
     grad_down_out,
@@ -453,7 +456,33 @@
     send_sems,
     recv_sems,
     out_sems,
+    tokens,
+    target,
+    gate_weight,
+    up_weight,
+    down_weight,
+    probe_gate,
+    probe_up,
+    probe_down,
+    in_sems,
 ):
+    loads = [
+        pltpu.make_async_copy(src, dst, in_sems.at[index])
+        for index, (src, dst) in enumerate(
+            (
+                (tokens_in, tokens),
+                (target_in, target),
+                (gate_weight_in, gate_weight),
+                (up_weight_in, up_weight),
+                (probe_gate_in, probe_gate),
+                (probe_up_in, probe_up),
+                (down_weight_in, down_weight),
+                (probe_down_in, probe_down),
+            )
+        )
+    ]
+    for load in loads:
+        load.start()
     copies = Copies(send_sems, recv_sems)
     core = lax.axis_index(CORE_AXIS)
     other_core = 1 - core
@@ -484,6 +513,8 @@
 
     own_rows = pl.ds(pl.multiple_of(core * HALF, HALF), HALF)
     other_rows = pl.ds(pl.multiple_of(other_core * HALF, HALF), HALF)
+    loads[0].wait()
+    loads[1].wait()
     x[h_here, y_here, core] = tokens[own_rows, :]
     tgt[core] = target[own_rows, :]
 
@@ -494,6 +525,8 @@
         dst[core, index, PADDED - 32 :] = jnp.zeros((32, FEATS), BF16)
         dst[core, index, :UNITS] = values
 
+    for load in loads[2:]:
+        load.wait()
     lay_out(proj, 0, gate_weight[...])
     lay_out(proj, 1, up_weight[...])
     lay_out(proj, 2, sign(probe_gate))
@@ -549,7 +582,7 @@
 
     x_gather.first(project_first)
     x_gather.middle()
-    x_gather.second(project_and_send)
+    x_gather.second(project_and_send, True)
     x_gather.last(project_and_send)
     each(4, row_sum.forward)
     each(4, row_sum.pair)
@@ -696,6 +729,19 @@
                     d_pre[place, z, 2 + index, rows, :] = value.astype(BF16)
 
             strips(one)
+
+    def down_grads(side):
+        plain_sum = jnp.zeros((PADDED, FEATS), F32)
+        along_sum = jnp.zeros((PADDED, FEATS), F32)
+        for place in range(RING):
+            plain = whole_units(hid, place, 0)
+            tangent = whole_units(hid, place, 1)
+            err_block = err[0, place, :, side].reshape(RING * HALF, FEATS)
+            dot_block = err[1, place, :, side].reshape(RING * HALF, FEATS)
+            plain_sum = plain_sum + dot_nn(plain, err_block)
+            along_sum = along_sum + dot_nn(tangent, err_block) + dot_nn(plain, dot_block)
+        grads_down[side, 0] = plain_sum
+        grads_down[side, 1] = along_sum
 
     hid_gather.pair(0)
     copies.arrived(down.at[other_core], near + 3, partner)
@@ -742,17 +788,20 @@
     err_gathers[0].middle()
     err_gathers[1].spread()
     err_gathers[1].outward()
-    err_gathers[0].second(turn_back(0))
+    err_gathers[0].second(turn_back(0), False)
     err_gathers[1].first(turn_back(1))
     err_gathers[1].middle()
     err_gathers[0].last(turn_back(0))
-    err_gathers[1].second(turn_back(1))
+    err_gathers[1].second(turn_back(1), False)
     back_sum.forward(0)
     err_gathers[1].last(turn_back(1))
     back_sum.pair(0)
     back_sum.forward(1)
+    down_grads(other_core)
+    copies.send(grads_down.at[other_core], grads_down_landed, near + 4, near + 4, partner)
     back_sum.finish(d_hid.at[x_here, z_here, 0], 0)
     back_gather.start(0)
+    down_grads(core)
     back_sum.pair(1)
     back_gather.pair(0)
     back_sum.finish(d_hid.at[x_here, z_here, 1], 1)
@@ -761,22 +810,6 @@
     back_gather.pair(1)
     coef_gather.finish(0)
 
-    def down_grads(side):
-        plain_sum = jnp.zeros((PADDED, FEATS), F32)
-        along_sum = jnp.zeros((PADDED, FEATS), F32)
-        for place in range(RING):
-            plain = whole_units(hid, place, 0)
-            tangent = whole_units(hid, place, 1)
-            err_block = err[0, place, :, side].reshape(RING * HALF, FEATS)
-            dot_block = err[1, place, :, side].reshape(RING * HALF, FEATS)
-            plain_sum = plain_sum + dot_nn(plain, err_block)
-            along_sum = along_sum + dot_nn(tangent, err_block) + dot_nn(plain, dot_block)
-        grads_down[side, 0] = plain_sum
-        grads_down[side, 1] = along_sum
-
-    down_grads(other_core)
-    copies.send(grads_down.at[other_core], grads_down_landed, near + 4, near + 4, partner)
-    down_grads(core)
 
     def tokens_of(place, side):
         return x[place, :, side].reshape(RING * HALF, FEATS)
@@ -902,7 +935,7 @@
             *[jax.ShapeDtypeStruct((UNITS, FEATS), F32)] * 6,
             jax.ShapeDtypeStruct((8, LANES), F32),
         ),
-        in_specs=[pl.BlockSpec(memory_space=pltpu.VMEM)] * 8,
+        in_specs=[pl.BlockSpec(memory_space=pl.ANY)] * 8,
         out_specs=[pl.BlockSpec(memory_space=pl.ANY)] * 6 + [pl.BlockSpec(memory_space=pltpu.VMEM)],
         scratch_shapes=[
             pltpu.VMEM((2, 4, PADDED, FEATS), BF16),
@@ -934,6 +967,8 @@
             pltpu.SemaphoreType.DMA((SENDS,)),
             pltpu.SemaphoreType.DMA((ARRIVALS,)),
             pltpu.SemaphoreType.DMA((6,)),
+            *[pltpu.VMEM(operand.shape, operand.dtype) for operand in operands],
+            pltpu.SemaphoreType.DMA((8,)),
         ],
         compiler_params=pltpu.CompilerParams(
             collective_id=0, has_side_effects=True, vmem_limit_bytes=60 * 1024 * 1024

time: 163 us -> 161 us (0.988)
  Pallas kernels: 161 us -> 159 us
    pallas_call x1, Pallas kernels: 157 us -> 155 us  [whole_step(): pl.pallas_call(step_kernel, out_shape=(*[jax.ShapeDtypeStruct((UNITS, FEA...]
where the time goes in v6:
time: 161 us; the launch traced here: 160 us
  Pallas kernels  159 us (99%)
    pallas_call x1, Pallas kernels, whole_step(): pl.pallas_call(step_kernel, out_shape=(*[jax.ShapeDtypeStruct((UNITS, FEA...  155 us
    pallas_call x1, Pallas kernels, update(): pl.pallas_call(update_kernel, out_shape=[jax.ShapeDtypeStruct((UNITS, FEA...  4.31 us

profile of v6, /device:TPU:32, one launch (start us, length us, event | category | flops | bytes accessed | tf_op | source)
XLA Modules:
  0.0 160.0 jit_solution(7275556798059079091)
XLA Ops:
  0.6 155.0 %shard_map.205 = (f32[344,256]{1,0:T(8,128)}, f32[344,256]{1,0:T(8,128)}, f32[344,256]{1,0:T(8,128)}, f32[344,256]{1,0:T(8,128)}, f32[344,256]{1,0:T(8,128)}, /*index=5*/f32[344,256]{1,0:T(8,128)}, f32[8,128]{1,0:T(8,128)}) custom-call(bf16[128,256]{1,0:T(8,128)(2,1)} %tokens_in.1, bf16[128,256]{1,0:T(8,128)(2,1)} %target_in.1, bf16[344,256]{1,0:T(8,128)(2,1)} %bitcast.20, ...), custom_call_target="tpu_custom_call" | custom-call | tf_op jit(solution)/shard_map/pallas_call | solution.py:932
  155.6 4.3 %shard_map.206 = (f32[344,256]{1,0:T(8,128)}, f32[344,256]{1,0:T(8,128)}, f32[344,256]{1,0:T(8,128)}, f32[344,256]{1,0:T(8,128)}, f32[344,256]{1,0:T(8,128)}, /*...) custom-call(f32[8,128]{1,0:T(8,128)} %get-tuple-element.25.sums, ...), custom_call_target="tpu_custom_call" | custom-call | tf_op jit(solution)/shard_map/pallas_call | solution.py:1016
